TPU v7x, 256 devices: a whole 4x4x8 slice. The times are simulated.
256 devices in a mesh: rep: 32 (over z, y), nodes: 8 (over x, core).
Axes of the slice: x: 4, y: 4, z: 8, core: 2. Of those that a mesh axis runs over, the one named last changes fastest.
Arguments:
- adjacency: bfloat16 [16384, 16384], P('nodes')
- features: bfloat16 [16384, 128], P(('nodes', 'rep'))
- w_one: float32 [128, 256], replicated
- w_two: float32 [256, 172], replicated
- labels: int32 [16384], P(('nodes', 'rep'))
- label_mask: int32 [16384], P(('nodes', 'rep'))
Outputs:
- output 1: float32 [], replicated
- output 2: float32 [128, 256], replicated
- output 3: float32 [256, 172], replicated
All inputs are finite; a program needn't handle non-finite values.
Results may differ from a plain program's by a relative error of at most 0.001.
Values are sent between devices in bfloat16 or wider.
A program may use at most 768 MiB of HBM per device.

v0:
```python
import jax
import jax.numpy as jnp
from jax import lax
from jax.sharding import PartitionSpec as P


def solution(mesh):
    rep_size = mesh.shape["rep"]
    node_size = mesh.shape["nodes"]
    all_axes = ("rep", "nodes")

    def local_step(adj_rows, features, w_one, w_two, labels, label_mask):
        rows_dev = features.shape[0]
        group_rows_n = adj_rows.shape[0]
        num_classes = w_two.shape[1]
        adj_split = adj_rows.reshape(group_rows_n, node_size, rep_size, rows_dev)
        adj_mine = lax.dynamic_index_in_dim(adj_split, lax.axis_index("rep"), axis=2, keepdims=False)

        def aggregate(values):
            gathered = lax.all_gather(values, "nodes")
            partial_sum = jnp.einsum("ajb,jbf->af", adj_mine, gathered, preferred_element_type=jnp.float32)
            return lax.psum_scatter(partial_sum, "rep", scatter_dimension=0, tiled=True)

        def aggregate_t(grad_rows):
            group_grads = lax.all_gather(grad_rows, "rep", tiled=True)
            partial_sum = jnp.einsum("ajb,af->jbf", adj_mine, group_grads, preferred_element_type=jnp.float32)
            return lax.psum_scatter(partial_sum, "nodes", scatter_dimension=0, tiled=False)

        w_one_b = w_one.astype(jnp.bfloat16)
        w_two_b = w_two.astype(jnp.bfloat16)
        y_one = jnp.dot(features, w_one_b, preferred_element_type=jnp.float32).astype(jnp.bfloat16)
        z_one = aggregate(y_one)
        h_one = jnp.maximum(z_one, 0.0).astype(jnp.bfloat16)
        y_two = jnp.dot(h_one, w_two_b, preferred_element_type=jnp.float32).astype(jnp.bfloat16)
        z_two = aggregate(y_two)
        log_probs = jax.nn.log_softmax(z_two, axis=-1)
        onehot = (labels[:, None] == jnp.arange(num_classes)[None, :]).astype(jnp.float32)
        mask_f = label_mask.astype(jnp.float32)
        local_sums = jnp.stack([-jnp.sum(mask_f * jnp.sum(onehot * log_probs, axis=-1)), jnp.sum(mask_f)])
        global_sums = lax.psum(local_sums, all_axes)
        loss_value = global_sums[0] / global_sums[1]
        g_two = ((jnp.exp(log_probs) - onehot) * (mask_f / global_sums[1])[:, None]).astype(jnp.bfloat16)
        dy_two = aggregate_t(g_two).astype(jnp.bfloat16)
        dw_two = lax.psum(jnp.einsum("vh,vc->hc", h_one, dy_two, preferred_element_type=jnp.float32), all_axes)
        dh_one = jnp.einsum("vc,hc->vh", dy_two, w_two_b, preferred_element_type=jnp.float32)
        g_one = jnp.where(z_one > 0, dh_one, 0.0).astype(jnp.bfloat16)
        dy_one = aggregate_t(g_one).astype(jnp.bfloat16)
        dw_one = lax.psum(jnp.einsum("vf,vh->fh", features, dy_one, preferred_element_type=jnp.float32), all_axes)
        return loss_value, dw_one, dw_two

    row_spec = P(("nodes", "rep"))
    return jax.shard_map(local_step, mesh=mesh, in_specs=(P("nodes", None), P(("nodes", "rep"), None), P(), P(), row_spec, row_spec), out_specs=(P(), P(), P()), check_vma=False)
```

profile of v0, /device:TPU:1, one launch (start us, length us, event | category | flops | bytes accessed | tf_op | source)
XLA Modules:
  0.0 1123.5 jit_solution(12468803951422898711)
XLA Ops:
  7.2 0.0 copy-start
  7.2 0.0 reduce-scatter.5.cloned.1.call-start
  7.2 0.7 copy-done
  7.9 1.0 convolution_convert_fusion.1
  8.9 15.8 %all-gather = bf16[512,256]{1,0:T(8,128)(2,1)S(1)} all-gather(bf16[64,256]{1,0:T(8,128)(2,1)S(1)} %convolution_convert_fusion.1), channel_id=2, replica_groups=mesh['rep'=32,'nodes'=8] {'nodes'}, dimensions={0}, use_global_device_ids=true | all-gather | bytes 294912 | tf_op jit(solution)/shard_map/all_gather | solution.py:20
  24.8 86.6 %copy.11 = bf16[2048,16384]{0,1:T(8,128)(2,1)} copy(bf16[2048,16384]{1,0:T(8,128)(2,1)} %param.6) | data formatting | bytes 134217728 | tf_op args[0]
  111.4 3.7 convolution_bitcast_fusion.1
  115.1 0.0 reduce-scatter.5.cloned.1.call-update
  115.1 0.0 reduce-scatter.7.cloned.1.call-start
  115.1 214.0 %reduce-scatter.5.cloned.1.call-done = f32[64,256]{1,0:T(8,128)} async-done(((f32[2048,256]{1,0:T(8,128)}), f32[64,256]{1,0:T(8,128)}) %reduce-scatter.5.cloned.1.call-update) | async-done | bytes 65552 | tf_op jit(solution)/shard_map/reduce_scatter | solution.py:22
  329.1 0.0 copy-done.1
  329.1 1.0 convolution_convert_fusion
  330.1 18.9 %all-gather.1 = bf16[512,172]{1,0:T(8,128)(2,1)S(1)} all-gather(bf16[64,172]{1,0:T(8,128)(2,1)S(1)} %convolution_convert_fusion), channel_id=3, replica_groups=mesh['rep'=32,'nodes'=8] {'nodes'}, dimensions={0}, use_global_device_ids=true | all-gather | bytes 198144 | tf_op jit(solution)/shard_map/all_gather | solution.py:20
  349.0 3.7 convolution_bitcast_fusion
  352.7 0.0 reduce-scatter.7.cloned.1.call-update
  352.7 0.0 reduce-scatter.9.cloned.1.call-start
  352.8 210.6 %reduce-scatter.7.cloned.1.call-done = f32[64,172]{1,0:T(8,128)} async-done(((f32[2048,172]{1,0:T(8,128)}), f32[64,172]{1,0:T(8,128)}) %reduce-scatter.7.cloned.1.call-update) | async-done | bytes 44048 | tf_op jit(solution)/shard_map/reduce_scatter | solution.py:22
  563.4 0.9 reduce_max.10
  564.3 1.0 exponential_reduce_fusion
  565.4 0.0 copy-done.4
  565.4 1.0 select_reduce_fusion
  566.4 0.0 copy-done.5
  566.4 0.6 multiply_reduce_fusion
  567.7 0.7 pad_maximum_fusion
  568.4 79.6 %psum.21 = f32[2]{0:T(128)S(1)} all-reduce(f32[2]{0:T(128)S(1)} %pad_maximum_fusion), channel_id=1, replica_groups=mesh['rep'=32,'nodes'=8] {'rep','nodes'}, use_global_device_ids=true, to_apply=%region_7.8 | all-reduce | flops 2 | bytes 16 | tf_op jit(solution)/shard_map/psum | solution.py:40
  648.0 0.6 fusion.29
  648.6 0.6 convert_divide_fusion
  649.3 0.9 multiply_convert_fusion
  650.2 37.8 %all_gather.22 = bf16[2048,172]{1,0:T(8,128)(2,1)S(1)} all-gather(bf16[64,172]{1,0:T(8,128)(2,1)S(1)} %multiply_convert_fusion), channel_id=1, replica_groups=mesh['rep'=32,'nodes'=8] {'rep'}, dimensions={0}, use_global_device_ids=true | all-gather | bytes 726528 | tf_op jit(solution)/shard_map/all_gather | solution.py:25
  688.0 3.1 fusion.2
  691.1 0.0 reduce-scatter.9.cloned.1.call-update
  691.1 0.0 all-gather.4.cloned.1.call-start
  691.2 38.9 %reduce-scatter.9.cloned.1.call-done = f32[1,64,172]{2,1,0:T(8,128)} async-done(((f32[8,64,172]{2,1,0:T(8,128)}), f32[1,64,172]{2,1,0:T(8,128)}) %reduce-scatter.9.cloned.1.call-update) | async-done | bytes 44048 | tf_op jit(solution)/shard_map/reduce_scatter | solution.py:27
  730.1 1.6 fusion.10
  731.7 0.0 all-gather.4.cloned.1.call-update
  731.8 0.0 reduce-scatter.11.cloned.1.call-start
  731.8 73.7 %all-gather.4.cloned.1.call-done = bf16[2048,256]{1,0:T(8,128)(2,1)} async-done(((bf16[64,256]{1,0:T(8,128)(2,1)}), bf16[2048,256]{1,0:T(8,128)(2,1)}) %all-gather.4.cloned.1.call-update) | async-done | bytes 1048592 | tf_op jit(solution)/shard_map/all_gather | solution.py:25
  805.5 3.4 fusion
  808.9 0.0 reduce-scatter.11.cloned.1.call-update
  808.9 0.0 all-reduce.3.cloned.1.call-start
  809.0 0.0 copy-done.3
  809.0 0.9 fusion.17
  809.9 33.4 %reduce-scatter.11.cloned.1.call-done = f32[1,64,256]{2,1,0:T(8,128)} async-done(((f32[8,64,256]{2,1,0:T(8,128)}), f32[1,64,256]{2,1,0:T(8,128)}) %reduce-scatter.11.cloned.1.call-update) | async-done | bytes 65552 | tf_op jit(solution)/shard_map/reduce_scatter | solution.py:27
  843.3 1.7 convolution_bitcast_fusion.2
  845.0 0.0 all-reduce.3.cloned.1.call-update
  846.4 265.9 %all-reduce.3.cloned.1.call-done = (f32[128,256]{0,1:T(8,128)}, f32[256,172]{0,1:T(8,128)}) async-done(((f32[128,256]{0,1:T(8,128)}, f32[256,172]{0,1:T(8,128)}), (f32[128,256]{0,1:T(8,128)}, f32[256,172]{0,1:T(8,128)})) %all-reduce.3.cloned.1.call-update) | async-done | bytes 307216 | tf_op jit(solution)/shard_map/psum | solution.py:48
  1112.3 1.7 copy.12
  1113.9 1.6 copy.15
  (7 shorter events, 0.0 us)
Async XLA Ops:
  7.2 0.7 copy-start
  7.2 321.9 %reduce-scatter.5.cloned.1.call-start = ((), (), s32[]{:S(2)}) async-start(), calls=%async_computation.4 | async-start | bytes 2162688 | tf_op jit(solution)/shard_map/reduce_scatter | solution.py:22
  115.1 214.0 %copy-start.1 = (f32[256,172]{0,1:T(8,128)S(1)}, f32[256,172]{0,1:T(8,128)}, u32[]{:S(2)}) copy-start(f32[256,172]{0,1:T(8,128)} %param.9) | copy-start | bytes 528388
  115.1 448.3 %reduce-scatter.7.cloned.1.call-start = ((), (), s32[]{:S(2)}) async-start(), calls=%async_computation.5 | async-start | bytes 2162688 | tf_op jit(solution)/shard_map/reduce_scatter | solution.py:22
  352.7 212.7 %copy-start.4 = (s32[64]{0:T(128)S(1)}, s32[64]{0:T(128)}, u32[]{:S(2)}) copy-start(s32[64]{0:T(128)} %param.10) | copy-start | bytes 772
  352.7 213.7 %copy-start.5 = (s32[64]{0:T(128)S(1)}, s32[64]{0:T(128)}, u32[]{:S(2)}) copy-start(s32[64]{0:T(128)} %param.11) | copy-start | bytes 772
  352.7 377.4 %reduce-scatter.9.cloned.1.call-start = ((), (), s32[]{:S(2)}) async-start(), calls=%async_computation.6 | async-start | bytes 589824 | tf_op jit(solution)/shard_map/reduce_scatter | solution.py:27
  688.0 42.1 %copy-start.2 = (f32[64,256]{1,0:T(8,128)S(1)}, f32[64,256]{1,0:T(8,128)}, u32[]{:S(2)}) copy-start(f32[64,256]{1,0:T(8,128)} %reduce-scatter.5.cloned.1.call-done) | copy-start | bytes 196612
  691.1 114.4 %all-gather.4.cloned.1.call-start = ((), (), s32[]{:S(2)}) async-start(), calls=%async_computation.7 | async-start | bytes 1081344 | tf_op jit(solution)/shard_map/all_gather | solution.py:25
  731.8 77.2 %copy-start.3 = (f32[1,64,172]{2,1,0:T(8,128)S(1)}, f32[1,64,172]{2,1,0:T(8,128)}, u32[]{:S(2)}) copy-start(f32[1,64,172]{2,1,0:T(8,128)} %reduce-scatter.9.cloned.1.call-done) | copy-start | bytes 132100
  731.8 111.5 %reduce-scatter.11.cloned.1.call-start = ((), (), s32[]{:S(2)}) async-start(), calls=%async_computation.8 | async-start | bytes 589824 | tf_op jit(solution)/shard_map/reduce_scatter | solution.py:27
  808.9 303.4 %all-reduce.3.cloned.1.call-start = ((), (), s32[]{:S(2)}) async-start(), calls=%async_computation.9 | async-start | bytes 622592 | tf_op jit(solution)/shard_map/psum | solution.py:48
Sparse Core Ops, SparseCore 0:
  115.2 213.8 reduce-scatter.4
  352.8 210.4 reduce-scatter.6
  691.3 38.8 reduce-scatter.8
  733.1 72.3 all-gather.3
  809.0 34.2 reduce-scatter.10
  849.3 262.9 all-reduce.2
where the time goes:
time: 1130 us; the launch traced here: 1120 us
  waiting for transfers between devices  837 us (74%)
  blocking collectives  152 us (13%)
  local copies, waits for them, and re-layouts  91.2 us (8%)
  matrix products  20 us (2%)
  between operations  17.4 us (2%)
    reduce_scatter x2, waiting for transfers between devices, aggregate(): return lax.psum_scatter(partial_sum, 'rep', scatter_dimension=0, tiled=True)  425 us
    psum x1, waiting for transfers between devices, local_step(): lax.psum(jnp.einsum('vf,vh->fh', features, dy_one, preferred_element_type...  266 us
    unnamed x15, local copies, waits for them, and re-layouts  90.6 us
    psum x1, blocking collectives, local_step(): global_sums = lax.psum(local_sums, all_axes)  79.6 us
    all_gather x1, waiting for transfers between devices, aggregate_t(): group_grads = lax.all_gather(grad_rows, 'rep', tiled=True)  73.7 us
    reduce_scatter x2, waiting for transfers between devices, aggregate_t(): lax.psum_scatter(partial_sum, 'nodes', scatter_dimension=0, tiled=False)  72.4 us
    all_gather x1, blocking collectives, aggregate_t(): group_grads = lax.all_gather(grad_rows, 'rep', tiled=True)  37.8 us
    all_gather x2, blocking collectives, aggregate(): gathered = lax.all_gather(values, 'nodes')  34.8 us
  transfers between devices with their start and end apart: 6, of which 6 were waited for; matrix products, arithmetic and copies ran while one was open for 0% of the time, Pallas kernels for 0%

commit v1 on v0

v1 whole, which is shorter than its diff:
```python
import functools

import jax
import jax.numpy as jnp
from jax import lax
from jax.experimental import pallas as pl
from jax.experimental.pallas import tpu as pltpu
from jax.sharding import PartitionSpec as P

BF = jnp.bfloat16
F32 = jnp.float32
BLK = 64
NEG = -1e30


def ring_order(n):
    return sorted(range(1, n), key=lambda d: (min(d, n - d), d))


def step_kernel(ZN, YN, XN, a_hbm, x_ref, w1_ref, w2_ref, lab_ref, msk_ref, loss_ref, dw1_ref, dw2_ref,
                af, ac, ab, at, xg, yg, y2g, g2g, g1g, zp, zr, dp, dr, ds_, dx, pay, payd, payx, payy, payz,
                mt, mz, mx, my, mc, z1s, h1s, y2pad, w2p,
                sem_af, sem_ab, zs, zrv, as_, arv, cs, crv, rs, rrv, ms, mrv, fs, frv):
    rep_n, node_n = ZN * YN, 2 * XN
    r, i = lax.axis_index("rep"), lax.axis_index("nodes")
    z, y = r // YN, lax.rem(r, YN)
    x, c = i // 2, lax.rem(i, 2)
    classes = w2_ref.shape[1]
    hidden = w1_ref.shape[1]
    zero = jnp.int32(0)

    def dev(dz=0, dy=0, dx_=0, dc=0):
        zz = lax.rem(z + dz, ZN)
        yy = lax.rem(y + dy, YN)
        xx = lax.rem(x + dx_, XN)
        cc = lax.rem(c + dc, 2)
        return {"rep": zz * YN + yy, "nodes": xx * 2 + cc}

    z_order, y_order, x_order = ring_order(ZN), ring_order(YN), ring_order(XN)
    peers = [dev(dz=d) for d in z_order] + [dev(dy=d) for d in y_order] + [dev(dx_=d) for d in x_order] + [dev(dc=1)]

    rows_z = YN * BLK
    n_q = node_n * ZN

    @pl.loop(0, n_q)
    def _(q):
        pltpu.make_async_copy(
            a_hbm.at[pl.ds(pl.multiple_of(z * rows_z, rows_z), rows_z),
                     pl.ds(pl.multiple_of(q * (YN * BLK) + (y // 2) * 128, 128), 128)],
            af.at[:, pl.ds(pl.multiple_of(q * 128, 128), 128)], sem_af).start()

    @pl.loop(0, node_n)
    def _(j):
        pltpu.make_async_copy(
            a_hbm.at[:, pl.ds(pl.multiple_of(j * (rep_n * BLK) + (r // 2) * 128, 128), 128)],
            ab.at[j], sem_ab).start()

    barrier = pltpu.get_barrier_semaphore()
    for peer in peers:
        pl.semaphore_signal(barrier, inc=1, device_id=peer, device_id_type=pl.DeviceIdType.MESH)

    own = pl.ds(pl.multiple_of((i * ZN + z) * BLK, BLK), BLK)
    xg[own, :] = x_ref[...]
    w2p[...] = jnp.zeros_like(w2p)
    w2p[:, :classes] = w2_ref[...].astype(BF)
    mask_row = msk_ref[...].astype(F32)
    mt[...] = jnp.broadcast_to(jnp.sum(mask_row, axis=1, keepdims=True), mt.shape)
    pl.semaphore_wait(barrier, len(peers))

    pending = []

    def send(src, dst, ssem, rsem, device):
        cp = pltpu.make_async_remote_copy(src_ref=src, dst_ref=dst, send_sem=ssem, recv_sem=rsem,
                                          device_id=device, device_id_type=pl.DeviceIdType.MESH)
        cp.start()
        pending.append(cp)
        return cp

    def gather(g, slot, axis_n, axis_order, peer_of, me, fillers=()):
        fillers = list(fillers)
        zc = {d: send(slot(z, me), slot(z, me), zs.at[g, d], zrv.at[g, d], dev(dz=d)) for d in z_order}
        axc = {}

        def spread(zk, k):
            for e in axis_order:
                axc[k, e] = send(slot(zk, me), slot(zk, me), as_.at[g, k, e], arv.at[g, k, e], peer_of(e))

        spread(z, 0)
        for d in z_order:
            if fillers:
                fillers.pop(0)()
            zc[d].wait_recv()
            spread(lax.rem(z + ZN - d, ZN), d)
        while fillers:
            fillers.pop(0)()
        return axc

    def exchange_small(k, src, buf, order, peer_of):
        return [send(src, buf.at[e], ms.at[k, e], mrv.at[k, e], peer_of(e)) for e in order]

    def compress():
        pltpu.make_async_copy(af, af, sem_af).wait()

        @pl.loop(0, n_q // 2)
        def _(p):
            even = af[:, pl.ds(pl.multiple_of(p * 256, 256), 128)]
            odd = af[:, pl.ds(pl.multiple_of(p * 256 + 128, 128), 128)]
            out = pl.ds(pl.multiple_of(p * 128, 128), 128)

            @pl.when(lax.rem(y, 2) == 0)
            def _():
                ac[:, out] = jnp.concatenate([even[:, :BLK], odd[:, :BLK]], axis=1)

            @pl.when(lax.rem(y, 2) == 1)
            def _():
                ac[:, out] = jnp.concatenate([even[:, BLK:], odd[:, BLK:]], axis=1)

    def transpose_part(lo, hi):
        def run():
            @pl.loop(lo, hi)
            def _(j):
                src_j = lax.rem(j, XN) * 2 + j // XN
                t = ab[src_j].T
                rows = pl.ds(pl.multiple_of(j * BLK, BLK), BLK)

                @pl.when(lax.rem(r, 2) == 0)
                def _():
                    at[rows, :] = t[:BLK]

                @pl.when(lax.rem(r, 2) == 1)
                def _():
                    at[rows, :] = t[BLK:]
        return run

    def wait_ab():
        pltpu.make_async_copy(ab, ab, sem_ab).wait()

    fill = [compress, wait_ab] + [transpose_part(k, k + 1) for k in range(node_n)]

    def fwd_gather(g, buf, fillers=()):
        def slot(zk, xk):
            return buf.at[pl.ds(pl.multiple_of(((xk * 2 + c) * ZN + zk) * BLK, BLK), BLK), :]

        axc = gather(g, slot, XN, x_order, lambda e: dev(dx_=e), x, fillers)
        core = []

        def line(xk):
            return buf.at[pl.ds(pl.multiple_of((xk * 2 + c) * ZN * BLK, ZN * BLK), ZN * BLK), :]

        core.append(send(line(x), line(x), cs.at[g, 0], crv.at[g, 0], dev(dc=1)))
        for e in x_order:
            for k in [0] + z_order:
                axc[k, e].wait_recv()
            xk = lax.rem(x + XN - e, XN)
            core.append(send(line(xk), line(xk), cs.at[g, e], crv.at[g, e], dev(dc=1)))
        for cp in core:
            cp.wait_recv()

    def fwd_reduce(g, buf):
        part = jnp.dot(ac[...], buf[...], preferred_element_type=F32)
        for k in range(YN):
            zp[g, k] = part[k * BLK:(k + 1) * BLK]
        cps = [send(zp.at[g, lax.rem(y + e, YN)], zr.at[g, e], rs.at[g, e], rrv.at[g, e], dev(dy=e)) for e in y_order]
        total = zp[g, y]
        for e, cp in zip(y_order, cps):
            cp.wait_recv()
            total = total + zr[g, e]
        return total

    mzc = exchange_small(0, mt.at[0], mz, z_order, lambda e: dev(dz=e))
    fwd_gather(0, xg, fill)
    b1 = w1_ref[...].astype(BF)
    chunk = min(512, xg.shape[0])

    @pl.loop(0, xg.shape[0] // chunk)
    def _(k):
        rows = pl.ds(pl.multiple_of(k * chunk, chunk), chunk)
        yg[rows, :] = jnp.dot(xg[rows, :], b1, preferred_element_type=F32).astype(BF)

    def small_sum(k, cps, order, buf, nxt):
        s = mt[k]
        for e, cp in zip(order, cps):
            cp.wait_recv()
            s = s + buf[e]
        mt[nxt] = s

    small_sum(0, mzc, z_order, mz, 1)
    mxc = exchange_small(1, mt.at[1], mx, x_order, lambda e: dev(dx_=e))
    z1 = fwd_reduce(0, yg)
    z1s[...] = z1
    h1 = jnp.maximum(z1, 0.0).astype(BF)
    h1s[...] = h1
    small_sum(1, mxc, x_order, mx, 2)
    myc = exchange_small(2, mt.at[2], my, y_order, lambda e: dev(dy=e))

    y2g[own, :] = jnp.dot(h1, w2p[...], preferred_element_type=F32).astype(BF)
    fwd_gather(1, y2g)
    small_sum(2, myc, y_order, my, 3)
    mcc = exchange_small(3, mt.at[3], mc, [1], lambda e: dev(dc=e))
    z2 = fwd_reduce(1, y2g)
    small_sum(3, mcc, [1], mc, 4)

    count = mt[4][:1, :1]
    diag = lax.broadcasted_iota(jnp.int32, (BLK, BLK), 0) == lax.broadcasted_iota(jnp.int32, (BLK, BLK), 1)
    labf = jnp.sum(jnp.where(diag, jnp.broadcast_to(lab_ref[...].astype(F32), (BLK, BLK)), 0.0), axis=1, keepdims=True)
    mskf = jnp.sum(jnp.where(diag, jnp.broadcast_to(mask_row, (BLK, BLK)), 0.0), axis=1, keepdims=True)
    lane = lax.broadcasted_iota(jnp.int32, z2.shape, 1)
    logits = jnp.where(lane < classes, z2, NEG)
    shifted = logits - jnp.max(logits, axis=1, keepdims=True)
    log_probs = shifted - jnp.log(jnp.sum(jnp.exp(shifted), axis=1, keepdims=True))
    onehot = jnp.where(lane.astype(F32) == labf, 1.0, 0.0)
    local_loss = -jnp.sum(mskf * jnp.sum(onehot * log_probs, axis=1, keepdims=True), axis=0, keepdims=True)
    g2 = ((jnp.exp(log_probs) - onehot) * (mskf / count)).astype(BF)

    def bwd(g, buf, value):
        def slot(zk, yk):
            return buf.at[pl.ds(pl.multiple_of((zk * YN + yk) * BLK, BLK), BLK), :]

        buf[pl.ds(pl.multiple_of(r * BLK, BLK), BLK), :] = value
        axc = gather(g, slot, YN, y_order, lambda e: dev(dy=e), y)
        for cp in axc.values():
            cp.wait_recv()
        b = g - 2
        part = jnp.dot(at[...], buf[...], preferred_element_type=F32)
        half = XN * BLK
        dp[b, 0] = part[:half]
        dp[b, 1] = part[half:]
        cp = send(dp.at[b, 1 - c], dr.at[b], cs.at[g, 0], crv.at[g, 0], dev(dc=1))
        cp.wait_recv()
        ds_[b] = dp[b, c] + dr[b]

        def mine(xk):
            return pl.ds(pl.multiple_of(xk * BLK, BLK), BLK)

        cps = [send(ds_.at[b, mine(lax.rem(x + e, XN))], dx.at[b, e], rs.at[g, e], rrv.at[g, e], dev(dx_=e)) for e in x_order]
        total = ds_[b, mine(x)]
        for e, cp in zip(x_order, cps):
            cp.wait_recv()
            total = total + dx[b, e]
        return total.astype(BF)

    d2 = bwd(2, g2g, g2)
    tdims = (((0,), (0,)), ((), ()))
    dw2 = lax.dot_general(h1s[...], d2, tdims, preferred_element_type=F32)
    dh1 = lax.dot_general(d2, w2p[...], (((1,), (1,)), ((), ())), preferred_element_type=F32)
    g1 = jnp.where(z1s[...] > 0, dh1, 0.0).astype(BF)
    d1 = bwd(3, g1g, g1)
    dw1 = lax.dot_general(x_ref[...], d1, tdims, preferred_element_type=F32)

    f_in = x_ref.shape[1]
    pay[0:f_in] = dw1[:, :128]
    pay[f_in:2 * f_in] = dw1[:, 128:]
    o2 = 2 * f_in
    pay[o2:o2 + hidden] = dw2[:, :128]
    row = lax.broadcasted_iota(jnp.int32, (hidden, 128), 0)
    lane2 = lax.broadcasted_iota(jnp.int32, (hidden, 128), 1)
    pay[o2 + hidden:o2 + 2 * hidden] = jnp.where(jnp.logical_and(row == 0, lane2 == 127), local_loss, dw2[:, 128:])
    n_rows = o2 + 2 * hidden
    rx = n_rows // node_n
    ry = rx // YN
    half = XN * rx

    cp = send(pay.at[pl.ds(pl.multiple_of((1 - c) * half, 8), half)], payd, fs.at[0, 0], frv.at[0, 0], dev(dc=1))
    cp.wait_recv()
    payd[...] = payd[...] + pay[pl.ds(pl.multiple_of(c * half, 8), half)]
    cps = [send(payd.at[pl.ds(pl.multiple_of(lax.rem(x + e, XN) * rx, 8), rx)], payx.at[e], fs.at[1, e], frv.at[1, e], dev(dx_=e)) for e in x_order]
    s = payd[pl.ds(pl.multiple_of(x * rx, 8), rx)]
    for e, cp in zip(x_order, cps):
        cp.wait_recv()
        s = s + payx[e]
    payx[0] = s
    cps = [send(payx.at[0, pl.ds(pl.multiple_of(lax.rem(y + e, YN) * ry, 8), ry)], payy.at[e], fs.at[2, e], frv.at[2, e], dev(dy=e)) for e in y_order]
    s = payx[0, pl.ds(pl.multiple_of(y * ry, 8), ry)]
    for e, cp in zip(y_order, cps):
        cp.wait_recv()
        s = s + payy[e]
    payz[z] = s
    cps = [send(payz.at[z], payz.at[z], fs.at[3, d], frv.at[3, d], dev(dz=d)) for d in z_order]
    for cp in cps:
        cp.wait_recv()
    s = payz[0]
    for k in range(1, ZN):
        s = s + payz[k]
    out = pay
    base = (c * XN + x) * rx
    for cp in pending:
        cp.wait_send()
    pending.clear()
    fin = af_out = ds_out = None
    fin = y2pad
    fin[pl.ds(pl.multiple_of(base + y * ry, 8), ry)] = s
    mine = fin.at[pl.ds(pl.multiple_of(base + y * ry, 8), ry)]
    cps = [send(mine, mine, fs.at[4, e], frv.at[4, e], dev(dy=e)) for e in y_order]
    for cp in cps:
        cp.wait_recv()
    mine = fin.at[pl.ds(pl.multiple_of(base, 8), rx)]
    cps = [send(mine, mine, fs.at[5, e], frv.at[5, e], dev(dx_=e)) for e in x_order]
    for cp in cps:
        cp.wait_recv()
    mine = fin.at[pl.ds(pl.multiple_of(c * half, 8), half)]
    cp = send(mine, mine, fs.at[6, 0], frv.at[6, 0], dev(dc=1))
    cp.wait_recv()
    dw1_ref[:, :128] = fin[0:f_in]
    dw1_ref[:, 128:] = fin[f_in:2 * f_in]
    dw2_ref[:, :128] = fin[o2:o2 + hidden]
    tail = fin[o2 + hidden:o2 + 2 * hidden]
    dw2_ref[:, 128:] = tail[:, :classes - 128]
    loss_ref[0, 0] = jnp.sum(tail[:1, 127:] / count)
    for cp in pending:
        cp.wait_send()


def solution(mesh):
    rep_n, node_n = mesh.shape["rep"], mesh.shape["nodes"]
    YN = 4 if rep_n == 32 else 2
    ZN = rep_n // YN
    XN = node_n // 2

    def local_step(adj, features, w_one, w_two, labels, mask):
        f_in, hidden = w_one.shape
        classes = w_two.shape[1]
        rows_g = adj.shape[0]
        cols_y = node_n * ZN * BLK
        n_pay = 2 * f_in + 2 * hidden
        rx = n_pay // node_n
        V = pltpu.VMEM
        D = pltpu.SemaphoreType.DMA
        scratch = dict(
            af=V((YN * BLK, node_n * ZN * 128), BF), ac=V((YN * BLK, cols_y), BF),
            ab=V((node_n, rows_g, 128), BF), at=V((node_n * BLK, rows_g), BF),
            xg=V((cols_y, f_in), BF), yg=V((cols_y, hidden), BF), y2g=V((cols_y, 256), BF),
            g2g=V((rows_g, 256), BF), g1g=V((rows_g, hidden), BF),
            zp=V((2, YN, BLK, 256), F32), zr=V((2, YN, BLK, 256), F32),
            dp=V((2, 2, XN * BLK, 256), F32), dr=V((2, XN * BLK, 256), F32), ds_=V((2, XN * BLK, 256), F32),
            dx=V((2, XN, BLK, 256), F32),
            pay=V((n_pay, 128), F32), payd=V((n_pay // 2, 128), F32), payx=V((XN, rx, 128), F32),
            payy=V((YN, rx // YN, 128), F32), payz=V((ZN, rx // YN, 128), F32),
            mt=V((5, 8, 128), F32), mz=V((ZN, 8, 128), F32), mx=V((XN, 8, 128), F32), my=V((YN, 8, 128), F32),
            mc=V((2, 8, 128), F32),
            z1s=V((BLK, hidden), F32), h1s=V((BLK, hidden), BF), y2pad=V((n_pay, 128), F32), w2p=V((hidden, 256), BF),
            sem_af=D, sem_ab=D,
            zs=D((4, ZN)), zrv=D((4, ZN)), as_=D((4, ZN, 4)), arv=D((4, ZN, 4)), cs=D((4, 4)), crv=D((4, 4)),
            rs=D((4, 4)), rrv=D((4, 4)), ms=D((4, ZN)), mrv=D((4, ZN)), fs=D((7, ZN)), frv=D((7, ZN)),
        )
        vm = pl.BlockSpec(memory_space=pltpu.VMEM)
        loss, dw1, dw2 = pl.pallas_call(
            functools.partial(step_kernel, ZN, YN, XN),
            out_shape=(jax.ShapeDtypeStruct((1, 1), F32), jax.ShapeDtypeStruct((f_in, hidden), F32),
                       jax.ShapeDtypeStruct((hidden, classes), F32)),
            in_specs=[pl.BlockSpec(memory_space=pl.ANY), vm, vm, vm, vm, vm],
            out_specs=(pl.BlockSpec(memory_space=pltpu.SMEM), vm, vm),
            scratch_shapes=list(scratch.values()),
            compiler_params=pltpu.CompilerParams(collective_id=0, has_side_effects=True, vmem_limit_bytes=60 * 2 ** 20),
            name="gcn_step",
        )(adj, features, w_one, w_two, labels.reshape(1, BLK), mask.reshape(1, BLK))
        return loss.reshape(()), dw1, dw2

    row_spec = P(("nodes", "rep"))
    return jax.shard_map(local_step, mesh=mesh, in_specs=(P("nodes", None), P(("nodes", "rep"), None), P(), P(), row_spec, row_spec),
                         out_specs=(P(), P(), P()), check_vma=False)
```

time: 1130 us -> 142 us (0.13)
  waiting for transfers between devices: 837 us -> 0 us
  blocking collectives: 152 us -> 0 us
  Pallas kernels: 0 us -> 134 us
  local copies, waits for them, and re-layouts: 91.2 us -> 5.05 us
  matrix products: 20 us -> 0 us
  between operations: 17.4 us -> 2.39 us
    reduce_scatter x4 -> x0, waiting for transfers between devices: 497 us -> none  [the longest x2 425 us: aggregate(): return lax.psum_scatter(partial_sum, 'rep', scatter_dimension=0, tiled=True)]
    psum x1 -> x0, waiting for transfers between devices: 266 us -> none  [local_step(): lax.psum(jnp.einsum('vf,vh->fh', features, dy_one, preferred_element_type...]
    pallas_call x0 -> x1, Pallas kernels: none -> 134 us  [local_step(): pl.pallas_call(functools.partial(step_kernel, ZN, YN, XN), out_shape=(jax...]
    unnamed x15 -> x3, local copies, waits for them, and re-layouts: 90.6 us -> 5.05 us
    psum x1 -> x0, blocking collectives: 79.6 us -> none  [local_step(): global_sums = lax.psum(local_sums, all_axes)]
    all_gather x1 -> x0, waiting for transfers between devices: 73.7 us -> none  [aggregate_t(): group_grads = lax.all_gather(grad_rows, 'rep', tiled=True)]
    all_gather x3 -> x0, blocking collectives: 72.6 us -> none  [the longest x1 37.8 us: aggregate_t(): group_grads = lax.all_gather(grad_rows, 'rep', tiled=True)]
    dot_general x9 -> x0, matrix products: 20 us -> none  [the longest x2 7.33 us: aggregate(): jnp.einsum('ajb,jbf->af', adj_mine, gathered, preferred_element_type=jnp....]
  transfers between devices with their start and end apart: 6 -> 0, of which waited for: 6 -> 0; matrix products, arithmetic and copies ran while one was open for 0% -> 0% of each run, Pallas kernels for 0% -> 0%
where the time goes in v1:
time: 142 us
  Pallas kernels  134 us (94%)
  local copies, waits for them, and re-layouts  5.05 us (4%)
  between operations  2.39 us (2%)
    pallas_call x1, Pallas kernels, local_step(): pl.pallas_call(functools.partial(step_kernel, ZN, YN, XN), out_shape=(jax...  134 us
    unnamed x3, local copies, waits for them, and re-layouts  5.05 us

profile of v1, /device:TPU:1, one launch (start us, length us, event | category | flops | bytes accessed | tf_op | source)
XLA Modules:
  0.0 141.6 jit_solution(18342769567633438722)
XLA Ops:
  0.6 1.7 %copy.9.w2_ref = f32[256,172]{1,0:T(8,128)} copy(f32[256,172]{0,1:T(8,128)} %param.9) | data formatting | bytes 352256 | tf_op args[3]
  2.4 134.2 %gcn_step.1 = (f32[1,1]{1,0:T(1,128)}, f32[128,256]{1,0:T(8,128)}, f32[256,172]{1,0:T(8,128)}) custom-call(bf16[2048,16384]{1,0:T(8,128)(2,1)} %a_hbm.1, bf16[64,128]{1,0:T(8,128)(2,1)} %x_ref.1, f32[128,256]{1,0:T(8,128)} %w1_ref.1, f32[256,172]{1,0:T(8,128)} %copy.9.w2_ref, s32[1,64]{1,0:T(1,128)} %bitcast.3, s32[1,64]{1,0:T(1,128)} %bitcast.4), custom_call_target="tpu_custom_call" | custom-call | tf_op jit(solution)/shard_map/gcn_step/pallas_call | solution.py:346
  136.6 1.7 %copy.10 = f32[256,172]{0,1:T(8,128)} copy(f32[256,172]{1,0:T(8,128)} %get-tuple-element.11) | data formatting | bytes 352256
  138.9 1.6 %copy.14 = f32[128,256]{1,0:T(8,128)} copy(f32[128,256]{1,0:T(8,128)} %get-tuple-element.16) | data formatting | bytes 262144

commit v2 on v0

v2 whole, which is shorter than its diff:
```python
import functools

import jax
import jax.numpy as jnp
from jax import lax
from jax.experimental import pallas as pl
from jax.experimental.pallas import tpu as pltpu
from jax.sharding import PartitionSpec as P

BF = jnp.bfloat16
F32 = jnp.float32
BLK = 64
NEG = -1e30


def ring_order(n):
    return sorted(range(1, n), key=lambda d: (min(d, n - d), d))


def pack(v):
    out = []
    lane = lax.broadcasted_iota(jnp.int32, (BLK // 2, 128), 1)
    for k in range(v.shape[0] // BLK):
        lo, hi = v[k * BLK:(k + 1) * BLK, :128], v[k * BLK:(k + 1) * BLK, 128:]
        out += [lo, jnp.where(lane < 64, hi[:BLK // 2], pltpu.roll(hi[BLK // 2:], 64, 1))]
    return jnp.concatenate(out, axis=0)


def unpack(p):
    lane = lax.broadcasted_iota(jnp.int32, (BLK // 2, 128), 1)
    t = p[BLK:]
    hi = jnp.concatenate([jnp.where(lane < 64, t, 0.0), jnp.where(lane < 64, pltpu.roll(t, 64, 1), 0.0)], axis=0)
    return jnp.concatenate([p[:BLK], hi], axis=1)


def step_kernel(ZN, YN, XN, names, *refs):
    R = dict(zip(names, refs))
    a_hbm, x_ref, w1_ref, w2_ref = R["a"], R["x"], R["w1"], R["w2"]
    af, ac, ab, at, w2p, mt = R["af"], R["ac"], R["ab"], R["at"], R["w2p"], R["mt"]
    rep_n, node_n = ZN * YN, 2 * XN
    r, i = lax.axis_index("rep"), lax.axis_index("nodes")
    z, y = r // YN, lax.rem(r, YN)
    x, c = i // 2, lax.rem(i, 2)
    classes, hidden = w2_ref.shape
    f_in = x_ref.shape[1]
    PB = 96

    def dev(dz=0, dy=0, dx=0, dc=0):
        return {"rep": lax.rem(z + dz, ZN) * YN + lax.rem(y + dy, YN),
                "nodes": lax.rem(x + dx, XN) * 2 + lax.rem(c + dc, 2)}

    def rows(k, n):
        return pl.ds(pl.multiple_of(k * n, n), n)

    z_order, y_order, x_order = ring_order(ZN), ring_order(YN), ring_order(XN)
    peers = [dev(dz=d) for d in z_order] + [dev(dy=d) for d in y_order] + [dev(dx=d) for d in x_order] + [dev(dc=1)]

    rows_z = YN * BLK
    n_q = node_n * ZN

    @pl.loop(0, n_q)
    def _(q):
        pltpu.make_async_copy(
            a_hbm.at[rows(z, rows_z), pl.ds(pl.multiple_of(q * (YN * BLK) + (y // 2) * 128, 128), 128)],
            af.at[:, rows(q, 128)], R["sem_af"]).start()

    @pl.loop(0, node_n)
    def _(j):
        pltpu.make_async_copy(
            a_hbm.at[:, pl.ds(pl.multiple_of(j * (rep_n * BLK) + (r // 2) * 128, 128), 128)],
            ab.at[j], R["sem_ab"]).start()

    barrier = pltpu.get_barrier_semaphore()
    for peer in peers:
        pl.semaphore_signal(barrier, inc=1, device_id=peer, device_id_type=pl.DeviceIdType.MESH)

    xg, yg, y2g, g2g, g1g = R["xg"], R["yg"], R["y2g"], R["g2g"], R["g1g"]
    own_f = (c * ZN + z) * XN + x
    xg[rows(own_f, BLK), :] = x_ref[...]
    w2p[...] = jnp.zeros_like(w2p)
    w2p[:classes, :] = w2_ref[...].astype(BF)
    b1 = w1_ref[...].astype(BF)
    mask_row = R["msk"][...].astype(F32)
    mt[0] = jnp.broadcast_to(jnp.sum(mask_row, axis=1, keepdims=True), mt.shape[1:])

    pltpu.make_async_copy(af, af, R["sem_af"]).wait()

    @pl.loop(0, n_q // 2)
    def _(p):
        xp = lax.rem(p, XN // 2)
        zk = lax.rem(p // (XN // 2), ZN)
        ck = p // (XN // 2 * ZN)
        q = (4 * xp + ck) * ZN + zk
        even, odd = af[:, rows(q, 128)], af[:, rows(q + 2 * ZN, 128)]
        out = rows(p, 128)

        @pl.when(lax.rem(y, 2) == 0)
        def _():
            ac[:, out] = jnp.concatenate([even[:, :BLK], odd[:, :BLK]], axis=1)

        @pl.when(lax.rem(y, 2) == 1)
        def _():
            ac[:, out] = jnp.concatenate([even[:, BLK:], odd[:, BLK:]], axis=1)

    pl.semaphore_wait(barrier, len(peers))

    pending = []

    def send(src, dst, ssem, rsem, device):
        cp = pltpu.make_async_remote_copy(src_ref=src, dst_ref=dst, send_sem=ssem, recv_sem=rsem,
                                          device_id=device, device_id_type=pl.DeviceIdType.MESH)
        cp.start()
        pending.append(cp)
        return cp

    def gather(g, buf, index, size, n, me, peer_of, done, fillers=()):
        fillers = list(fillers)
        half = size // 2
        zs, zr, ss, sr = R["zs"], R["zr"], R["ss"], R["sr"]

        def slot(zk, ak):
            return buf.at[rows(index(zk, ak), size)]

        def part(zk, ak, h):
            return buf.at[pl.ds(pl.multiple_of(index(zk, ak) * size + h * half, half), half)]

        def zof(k):
            return lax.rem(z + ZN - k, ZN)

        order = [0] + z_order
        zc = {d: send(slot(z, me), slot(z, me), zs.at[g, d], zr.at[g, d], dev(dz=d)) for d in z_order}
        near, far = {}, {}

        def spread(k):
            mine = slot(zof(k), me)
            near[k] = [send(mine, mine, ss.at[g, k, e], sr.at[g, k, e], peer_of(e)) for e in ([1, 3] if n == 4 else [1])]

        def relay(k):
            far[k] = []
            for h, cp in enumerate(near[k]):
                cp.wait_recv()
                if n == 4:
                    piece = part(zof(k), lax.rem(me + (3 if h == 0 else 1), n), h)
                    far[k].append(send(piece, piece, ss.at[g, k, 2 * h], sr.at[g, k, 2 * h], peer_of(1 if h == 0 else 3)))

        def finish(k):
            for cp in far[k]:
                cp.wait_recv()
            done(zof(k), k)

        steps = len(order)
        for s in range(steps + 2):
            if s < steps:
                if s:
                    if fillers:
                        fillers.pop(0)()
                    zc[order[s]].wait_recv()
                spread(order[s])
            if 1 <= s <= steps:
                relay(order[s - 1])
            if s >= 2:
                finish(order[s - 2])
        while fillers:
            fillers.pop(0)()

    def transpose_part(j):
        def run():
            if j == 0:
                pltpu.make_async_copy(ab, ab, R["sem_ab"]).wait()
            t = ab[(j % XN) * 2 + j // XN].T

            @pl.when(lax.rem(r, 2) == 0)
            def _():
                at[j * BLK:(j + 1) * BLK, :] = t[:BLK]

            @pl.when(lax.rem(r, 2) == 1)
            def _():
                at[j * BLK:(j + 1) * BLK, :] = t[BLK:]
        return run

    fill = [transpose_part(j) for j in range(node_n)]

    def unpack_rows(buf, first_block, n, out):
        for k in range(n):
            base = pl.multiple_of((first_block + k) * PB, 32)
            orow = pl.multiple_of((first_block + k) * BLK, BLK)
            t = buf[pl.ds(base + BLK, BLK // 2), :]
            out[pl.ds(orow, BLK), :128] = buf[pl.ds(base, BLK), :]
            out[pl.ds(orow, BLK // 2), 128:] = t
            out[pl.ds(orow + BLK // 2, BLK // 2), 128:] = jnp.concatenate([t[:, 64:], t[:, :64]], axis=1)

    zacc = R["zacc"]

    def fwd_gather(g, buf, size, prepare, fillers=()):
        late = []

        def line(ck, zk):
            return buf.at[rows(ck * ZN + zk, XN * size)]

        def add(ck, zk, first):
            k = ck * ZN + zk
            prepare(k)
            v = jnp.dot(ac[:, rows(k, XN * BLK)], yg[g, rows(k, XN * BLK), :], preferred_element_type=F32)
            if first:
                zacc[...] = v
            else:
                zacc[...] += v

        def partner():
            cp, zk = late.pop(0)
            cp.wait_recv()
            add(1 - c, zk, False)

        def done(zk, k):
            mine = line(c, zk)
            late.append((send(mine, mine, R["cs"].at[g, k], R["cr"].at[g, k], dev(dc=1)), zk))
            add(c, zk, k == 0)
            if len(late) > 1:
                partner()

        gather(g, buf, lambda zk, xk: (c * ZN + zk) * XN + xk, size, XN, x, lambda e: dev(dx=e), done, fillers)
        while late:
            partner()

    def fwd_reduce(g, packed):
        zp, zr = (R["zpp"], R["zrp"]) if packed else (R["zp"], R["zrw"])
        v = zacc[...]
        for k in range(YN):
            piece = v[k * BLK:(k + 1) * BLK]
            zp[k] = pack(piece) if packed else piece
        cps = [send(zp.at[lax.rem(y + e, YN)], zr.at[e], R["rs"].at[g, e], R["rr"].at[g, e], dev(dy=e)) for e in y_order]
        total = zp[y]
        for e, cp in zip(y_order, cps):
            cp.wait_recv()
            total = total + zr[e]
        return unpack(total) if packed else total

    def exchange_small(k, src, buf, order, peer_of):
        return [send(src, buf.at[e], R["ms"].at[k, e], R["mr"].at[k, e], peer_of(e)) for e in order]

    def small_sum(k, cps, order, buf, nxt):
        s = mt[k]
        for e, cp in zip(order, cps):
            cp.wait_recv()
            s = s + buf[e]
        mt[nxt] = s

    def y1_rows(k):
        rr = rows(k, XN * BLK)
        yg[0, rr, :] = jnp.dot(xg[rr, :], b1, preferred_element_type=F32).astype(BF)

    def y2_rows(k):
        unpack_rows(y2g, k * XN, XN, yg.at[1])

    mzc = exchange_small(0, mt.at[0], R["mz"], z_order, lambda e: dev(dz=e))
    fwd_gather(0, xg, BLK, y1_rows, fill[:node_n // 2])
    small_sum(0, mzc, z_order, R["mz"], 1)
    mxc = exchange_small(1, mt.at[1], R["mx"], x_order, lambda e: dev(dx=e))
    z1 = fwd_reduce(0, False)
    R["z1s"][...] = z1
    h1 = jnp.maximum(z1, 0.0).astype(BF)
    R["h1s"][...] = h1
    nt = (((1,), (1,)), ((), ()))
    y2 = lax.dot_general(h1, w2p[...], nt, preferred_element_type=F32)
    y2g[rows(own_f, PB), :] = pack(y2).astype(BF)
    small_sum(1, mxc, x_order, R["mx"], 2)
    myc = exchange_small(2, mt.at[2], R["my"], y_order, lambda e: dev(dy=e))
    fwd_gather(1, y2g, PB, y2_rows, fill[node_n // 2:])
    small_sum(2, myc, y_order, R["my"], 3)
    mcc = exchange_small(3, mt.at[3], R["mc"], [1], lambda e: dev(dc=e))
    z2 = fwd_reduce(1, True)
    small_sum(3, mcc, [1], R["mc"], 4)

    count = mt[4][:1, :1]
    diag = lax.broadcasted_iota(jnp.int32, (BLK, BLK), 0) == lax.broadcasted_iota(jnp.int32, (BLK, BLK), 1)
    labf = jnp.sum(jnp.where(diag, jnp.broadcast_to(R["lab"][...].astype(F32), (BLK, BLK)), 0.0), axis=1, keepdims=True)
    mskf = jnp.sum(jnp.where(diag, jnp.broadcast_to(mask_row, (BLK, BLK)), 0.0), axis=1, keepdims=True)
    lane = lax.broadcasted_iota(jnp.int32, z2.shape, 1)
    logits = jnp.where(lane < classes, z2, NEG)
    shifted = logits - jnp.max(logits, axis=1, keepdims=True)
    log_probs = shifted - jnp.log(jnp.sum(jnp.exp(shifted), axis=1, keepdims=True))
    onehot = jnp.where(lane.astype(F32) == labf, 1.0, 0.0)
    g2 = (jnp.exp(log_probs) - onehot) * (mskf / count)
    g2g[rows(r, PB), :] = pack(g2).astype(BF)
    local_loss = -jnp.sum(mskf * jnp.sum(onehot * log_probs, axis=1, keepdims=True), axis=0, keepdims=True)

    dacc = R["dacc"]

    def bwd(g, buf, size, packed, fillers=()):
        gu = R["gu"] if packed else buf

        def done(zk, k):
            if packed:
                unpack_rows(buf, zk * YN, YN, gu)
            rr = rows(zk, YN * BLK)
            v = jnp.dot(at[:, rr], gu[rr, :], preferred_element_type=F32)
            if k == 0:
                dacc[...] = v
            else:
                dacc[...] += v

        gather(g, buf, lambda zk, yk: zk * YN + yk, size, YN, y, lambda e: dev(dy=e), done, fillers)
        dp, dr, dsum, dx = (R["dpp"], R["drp"], R["dsp"], R["dxp"]) if packed else (R["dp"], R["dr"], R["ds"], R["dx"])
        for k in range(2):
            for j in range(XN):
                piece = dacc[(k * XN + j) * BLK:(k * XN + j + 1) * BLK]
                dp[k, j] = pack(piece) if packed else piece
        cp = send(dp.at[1 - c], dr, R["cs"].at[g, 0], R["cr"].at[g, 0], dev(dc=1))
        cp.wait_recv()
        dsum[...] = dp[c] + dr[...]
        cps = [send(dsum.at[lax.rem(x + e, XN)], dx.at[e], R["rs"].at[g, e], R["rr"].at[g, e], dev(dx=e)) for e in x_order]
        total = dsum[x]
        for e, cp in zip(x_order, cps):
            cp.wait_recv()
            total = total + dx[e]
        return (unpack(total) if packed else total).astype(BF)

    def all_reduce(t, pay, payd, payx, payy, payz, fin):
        n_rows = pay.shape[0]
        rx = n_rows // node_n
        ry = rx // YN
        half = XN * rx
        fs, fr = R["fs"], R["fr"]
        state = {}
        base = (c * XN + x) * rx

        def s0():
            state["cp"] = [send(pay.at[rows(1 - c, half)], payd, fs.at[t, 0, 0], fr.at[t, 0, 0], dev(dc=1))]

        def s1():
            state["cp"][0].wait_recv()
            payd[...] = payd[...] + pay[rows(c, half)]
            state["cp"] = [send(payd.at[rows(lax.rem(x + e, XN), rx)], payx.at[e], fs.at[t, 1, e], fr.at[t, 1, e], dev(dx=e)) for e in x_order]

        def s2():
            s = payd[rows(x, rx)]
            for e, cp in zip(x_order, state["cp"]):
                cp.wait_recv()
                s = s + payx[e]
            payx[0] = s
            state["cp"] = [send(payx.at[0, rows(lax.rem(y + e, YN), ry)], payy.at[e], fs.at[t, 2, e], fr.at[t, 2, e], dev(dy=e)) for e in y_order]

        def s3():
            s = payx[0, rows(y, ry)]
            for e, cp in zip(y_order, state["cp"]):
                cp.wait_recv()
                s = s + payy[e]
            payz[z] = s
            state["cp"] = [send(payz.at[z], payz.at[z], fs.at[t, 3, d], fr.at[t, 3, d], dev(dz=d)) for d in z_order]

        def s4():
            for cp in state["cp"]:
                cp.wait_recv()
            s = payz[0]
            for k in range(1, ZN):
                s = s + payz[k]
            mine = fin.at[pl.ds(pl.multiple_of(base + y * ry, 8), ry)]
            fin[pl.ds(pl.multiple_of(base + y * ry, 8), ry)] = s
            state["cp"] = [send(mine, mine, fs.at[t, 4, e], fr.at[t, 4, e], dev(dy=e)) for e in y_order]

        def s5():
            for cp in state["cp"]:
                cp.wait_recv()
            mine = fin.at[pl.ds(pl.multiple_of(base, 8), rx)]
            state["cp"] = [send(mine, mine, fs.at[t, 5, e], fr.at[t, 5, e], dev(dx=e)) for e in x_order]

        def s6():
            for cp in state["cp"]:
                cp.wait_recv()
            mine = fin.at[rows(c, half)]
            state["cp"] = [send(mine, mine, fs.at[t, 6, 0], fr.at[t, 6, 0], dev(dc=1))]

        def s7():
            state["cp"][0].wait_recv()

        return [s0, s1, s2, s3, s4, s5, s6, s7]

    d2 = bwd(2, g2g, PB, True)
    tn = (((0,), (0,)), ((), ()))
    dh1 = jnp.dot(d2, w2p[...], preferred_element_type=F32)
    g1g[rows(r, BLK), :] = jnp.where(R["z1s"][...] > 0, dh1, 0.0).astype(BF)
    R["d2s"][...] = d2
    ar2 = all_reduce(0, R["pay2"], R["payd2"], R["payx2"], R["payy2"], R["payz2"], R["fin2"])

    def make_dw2():
        dw2 = lax.dot_general(R["d2s"][...], R["h1s"][...], tn, preferred_element_type=F32)
        row = lax.broadcasted_iota(jnp.int32, (256, 128), 0)
        lane2 = lax.broadcasted_iota(jnp.int32, (256, 128), 1)
        R["pay2"][0:256] = jnp.where(jnp.logical_and(row == 255, lane2 == 127), local_loss, dw2[:, :128])
        R["pay2"][256:512] = dw2[:, 128:]
        ar2[0]()

    def nothing():
        pass

    d1 = bwd(3, g1g, BLK, False, [make_dw2, nothing, ar2[1], nothing, ar2[2], nothing, ar2[3]])
    dw1 = lax.dot_general(x_ref[...], d1, tn, preferred_element_type=F32)
    R["pay1"][0:f_in] = dw1[:, :128]
    R["pay1"][f_in:2 * f_in] = dw1[:, 128:]
    ar1 = all_reduce(1, R["pay1"], R["payd1"], R["payx1"], R["payy1"], R["payz1"], R["fin1"])
    for s in range(8):
        ar1[s]()
        if s < 4:
            ar2[4 + s]()
    fin1, fin2 = R["fin1"], R["fin2"]
    R["dw2"][:, :128] = fin2[0:classes]
    R["dw2"][:, 128:] = fin2[256:256 + classes]
    R["loss"][0, 0] = jnp.sum(fin2[255:256, 127:] / count)
    R["dw1"][:, :128] = fin1[0:f_in]
    R["dw1"][:, 128:] = fin1[f_in:2 * f_in]
    for cp in pending:
        cp.wait_send()


def solution(mesh):
    rep_n, node_n = mesh.shape["rep"], mesh.shape["nodes"]
    YN = 4
    ZN = rep_n // YN
    XN = node_n // 2

    def local_step(adj, features, w_one, w_two, labels, mask):
        f_in, hidden = w_one.shape
        classes = w_two.shape[1]
        rows_g = adj.shape[0]
        blocks_y = node_n * ZN
        V = pltpu.VMEM
        D = pltpu.SemaphoreType.DMA

        def reduce_bufs(t, n):
            rx = n // node_n
            return {f"pay{t}": V((n, 128), F32), f"payd{t}": V((n // 2, 128), F32), f"payx{t}": V((XN, rx, 128), F32),
                    f"payy{t}": V((YN, rx // YN, 128), F32), f"payz{t}": V((ZN, rx // YN, 128), F32), f"fin{t}": V((n, 128), F32)}

        scratch = dict(
            af=V((YN * BLK, blocks_y * 128), BF), ac=V((YN * BLK, blocks_y * BLK), BF),
            ab=V((node_n, rows_g, 128), BF), at=V((node_n * BLK, rows_g), BF),
            xg=V((blocks_y * BLK, f_in), BF), yg=V((2, blocks_y * BLK, 256), BF), y2g=V((blocks_y * 96, 128), BF),
            g2g=V((rep_n * 96, 128), BF), gu=V((rows_g, 256), BF), g1g=V((rows_g, hidden), BF),
            zacc=V((YN * BLK, 256), F32), dacc=V((node_n * BLK, 256), F32),
            zp=V((YN, BLK, 256), F32), zrw=V((YN, BLK, 256), F32), zpp=V((YN, 96, 128), F32), zrp=V((YN, 96, 128), F32),
            dp=V((2, XN, BLK, 256), F32), dr=V((XN, BLK, 256), F32), ds=V((XN, BLK, 256), F32), dx=V((XN, BLK, 256), F32),
            dpp=V((2, XN, 96, 128), F32), drp=V((XN, 96, 128), F32), dsp=V((XN, 96, 128), F32), dxp=V((XN, 96, 128), F32),
            mt=V((5, 8, 128), F32), mz=V((ZN, 8, 128), F32), mx=V((XN, 8, 128), F32), my=V((YN, 8, 128), F32),
            mc=V((2, 8, 128), F32),
            z1s=V((BLK, hidden), F32), h1s=V((BLK, hidden), BF), d2s=V((BLK, 256), BF), w2p=V((256, hidden), BF),
            sem_af=D, sem_ab=D,
            zs=D((4, 8)), zr=D((4, 8)), ss=D((4, 8, 4)), sr=D((4, 8, 4)), cs=D((4, 8)), cr=D((4, 8)),
            rs=D((4, 4)), rr=D((4, 4)), ms=D((4, 8)), mr=D((4, 8)), fs=D((2, 7, 8)), fr=D((2, 7, 8)),
        )
        scratch.update(reduce_bufs(1, 2 * f_in))
        scratch.update(reduce_bufs(2, 512))
        names = ["a", "x", "w1", "w2", "lab", "msk", "loss", "dw1", "dw2"] + list(scratch)
        vm = pl.BlockSpec(memory_space=pltpu.VMEM)
        loss, dw1, dw2 = pl.pallas_call(
            functools.partial(step_kernel, ZN, YN, XN, names),
            out_shape=(jax.ShapeDtypeStruct((1, 1), F32), jax.ShapeDtypeStruct((f_in, hidden), F32),
                       jax.ShapeDtypeStruct((classes, hidden), F32)),
            in_specs=[pl.BlockSpec(memory_space=pl.ANY), vm, vm, vm, vm, vm],
            out_specs=(pl.BlockSpec(memory_space=pltpu.SMEM), vm, vm),
            scratch_shapes=list(scratch.values()),
            compiler_params=pltpu.CompilerParams(collective_id=0, has_side_effects=True, vmem_limit_bytes=60 * 2 ** 20),
            name="gcn_step",
        )(adj, features, w_one, w_two.T, labels.reshape(1, BLK), mask.reshape(1, BLK))
        return loss.reshape(()), dw1, dw2.T

    row_spec = P(("nodes", "rep"))
    return jax.shard_map(local_step, mesh=mesh, in_specs=(P("nodes", None), P(("nodes", "rep"), None), P(), P(), row_spec, row_spec),
                         out_specs=(P(), P(), P()), check_vma=False)
```

time: 1130 us -> 175 us (0.15)
  waiting for transfers between devices: 837 us -> 0 us
  Pallas kernels: 0 us -> 168 us
  blocking collectives: 152 us -> 0 us
  local copies, waits for them, and re-layouts: 91.2 us -> 3.17 us
  matrix products: 20 us -> 0 us
  between operations: 17.4 us -> 2.46 us
    reduce_scatter x4 -> x0, waiting for transfers between devices: 497 us -> none  [the longest x2 425 us: aggregate(): return lax.psum_scatter(partial_sum, 'rep', scatter_dimension=0, tiled=True)]
    psum x1 -> x0, waiting for transfers between devices: 266 us -> none  [local_step(): lax.psum(jnp.einsum('vf,vh->fh', features, dy_one, preferred_element_type...]
    pallas_call x0 -> x1, Pallas kernels: none -> 168 us  [local_step(): pl.pallas_call(functools.partial(step_kernel, ZN, YN, XN, names), out_sha...]
    unnamed x15 -> x2, local copies, waits for them, and re-layouts: 90.6 us -> 3.17 us
    psum x1 -> x0, blocking collectives: 79.6 us -> none  [local_step(): global_sums = lax.psum(local_sums, all_axes)]
    all_gather x1 -> x0, waiting for transfers between devices: 73.7 us -> none  [aggregate_t(): group_grads = lax.all_gather(grad_rows, 'rep', tiled=True)]
    all_gather x3 -> x0, blocking collectives: 72.6 us -> none  [the longest x1 37.8 us: aggregate_t(): group_grads = lax.all_gather(grad_rows, 'rep', tiled=True)]
    dot_general x9 -> x0, matrix products: 20 us -> none  [the longest x2 7.33 us: aggregate(): jnp.einsum('ajb,jbf->af', adj_mine, gathered, preferred_element_type=jnp....]
  transfers between devices with their start and end apart: 6 -> 0, of which waited for: 6 -> 0; matrix products, arithmetic and copies ran while one was open for 0% -> 0% of each run, Pallas kernels for 0% -> 0%
where the time goes in v2:
time: 175 us; the launch traced here: 174 us
  Pallas kernels  168 us (96%)
  local copies, waits for them, and re-layouts  3.17 us (2%)
  between operations  2.46 us (1%)
    pallas_call x1, Pallas kernels, local_step(): pl.pallas_call(functools.partial(step_kernel, ZN, YN, XN, names), out_sha...  168 us

profile of v2, /device:TPU:1, one launch (start us, length us, event | category | flops | bytes accessed | tf_op | source)
XLA Modules:
  0.0 173.7 jit_solution(4727420808353536699)
XLA Ops:
  0.6 168.1 %gcn_step.1 = (f32[1,1]{1,0:T(1,128)}, f32[128,256]{1,0:T(8,128)}, f32[172,256]{1,0:T(8,128)}) custom-call(bf16[2048,16384]{1,0:T(8,128)(2,1)} %refs_0_.1, bf16[64,128]{1,0:T(8,128)(2,1)} %refs_1_.1, f32[128,256]{1,0:T(8,128)} %refs_2_.1, f32[172,256]{1,0:T(8,128)} %bitcast.6, s32[1,64]{1,0:T(1,128)} %bitcast.7, s32[1,64]{1,0:T(1,128)} %bitcast.8), custom_call_target="tpu_custom_call" | custom-call | tf_op jit(solution)/shard_map/gcn_step/pallas_call | solution.py:454
  169.4 1.6 copy.13
  171.0 1.6 copy.14

commit v3 on v2

--- a/solution.py
+++ b/solution.py
@@ -49,11 +49,14 @@
         return {"rep": lax.rem(z + dz, ZN) * YN + lax.rem(y + dy, YN),
                 "nodes": lax.rem(x + dx, XN) * 2 + lax.rem(c + dc, 2)}
 
+    def node_dev(e):
+        return {"rep": r, "nodes": lax.rem(i + e, node_n)}
+
     def rows(k, n):
         return pl.ds(pl.multiple_of(k * n, n), n)
 
     z_order, y_order, x_order = ring_order(ZN), ring_order(YN), ring_order(XN)
-    peers = [dev(dz=d) for d in z_order] + [dev(dy=d) for d in y_order] + [dev(dx=d) for d in x_order] + [dev(dc=1)]
+    peers = [dev(dz=d) for d in z_order] + [dev(dy=d) for d in y_order] + [node_dev(e) for e in range(1, node_n)]
 
     rows_z = YN * BLK
     n_q = node_n * ZN
@@ -85,22 +88,25 @@
 
     pltpu.make_async_copy(af, af, R["sem_af"]).wait()
 
-    @pl.loop(0, n_q // 2)
-    def _(p):
-        xp = lax.rem(p, XN // 2)
-        zk = lax.rem(p // (XN // 2), ZN)
-        ck = p // (XN // 2 * ZN)
-        q = (4 * xp + ck) * ZN + zk
-        even, odd = af[:, rows(q, 128)], af[:, rows(q + 2 * ZN, 128)]
-        out = rows(p, 128)
-
-        @pl.when(lax.rem(y, 2) == 0)
-        def _():
-            ac[:, out] = jnp.concatenate([even[:, :BLK], odd[:, :BLK]], axis=1)
-
-        @pl.when(lax.rem(y, 2) == 1)
-        def _():
-            ac[:, out] = jnp.concatenate([even[:, BLK:], odd[:, BLK:]], axis=1)
+    def select(lo):
+        @pl.loop(0, n_q // 8)
+        def _(step):
+            for u in range(4):
+                p = step * 4 + u
+                xp = lax.rem(p, XN // 2)
+                zk = lax.rem(p // (XN // 2), ZN)
+                ck = p // (XN // 2 * ZN)
+                q = (4 * xp + ck) * ZN + zk
+                even, odd = af[:, rows(q, 128)], af[:, rows(q + 2 * ZN, 128)]
+                ac[:, rows(p, 128)] = jnp.concatenate([even[:, lo:lo + BLK], odd[:, lo:lo + BLK]], axis=1)
+
+    @pl.when(lax.rem(y, 2) == 0)
+    def _():
+        select(0)
+
+    @pl.when(lax.rem(y, 2) == 1)
+    def _():
+        select(BLK)
 
     pl.semaphore_wait(barrier, len(peers))
 
@@ -113,72 +119,65 @@
         pending.append(cp)
         return cp
 
-    def gather(g, buf, index, size, n, me, peer_of, done, fillers=()):
-        fillers = list(fillers)
-        half = size // 2
+    def gather(g, buf, index, size, n, me, peer_of, done, hooks):
         zs, zr, ss, sr = R["zs"], R["zr"], R["ss"], R["sr"]
 
-        def slot(zk, ak):
-            return buf.at[rows(index(zk, ak), size)]
-
-        def part(zk, ak, h):
-            return buf.at[pl.ds(pl.multiple_of(index(zk, ak) * size + h * half, half), half)]
+        def slot(zk):
+            return buf.at[rows(index(zk, me), size)]
 
         def zof(k):
             return lax.rem(z + ZN - k, ZN)
 
-        order = [0] + z_order
-        zc = {d: send(slot(z, me), slot(z, me), zs.at[g, d], zr.at[g, d], dev(dz=d)) for d in z_order}
-        near, far = {}, {}
+        line = {}
 
         def spread(k):
-            mine = slot(zof(k), me)
-            near[k] = [send(mine, mine, ss.at[g, k, e], sr.at[g, k, e], peer_of(e)) for e in ([1, 3] if n == 4 else [1])]
-
-        def relay(k):
-            far[k] = []
-            for h, cp in enumerate(near[k]):
-                cp.wait_recv()
-                if n == 4:
-                    piece = part(zof(k), lax.rem(me + (3 if h == 0 else 1), n), h)
-                    far[k].append(send(piece, piece, ss.at[g, k, 2 * h], sr.at[g, k, 2 * h], peer_of(1 if h == 0 else 3)))
-
-        def finish(k):
-            for cp in far[k]:
-                cp.wait_recv()
-            done(zof(k), k)
-
-        steps = len(order)
-        for s in range(steps + 2):
-            if s < steps:
-                if s:
-                    if fillers:
-                        fillers.pop(0)()
-                    zc[order[s]].wait_recv()
-                spread(order[s])
-            if 1 <= s <= steps:
-                relay(order[s - 1])
-            if s >= 2:
-                finish(order[s - 2])
-        while fillers:
+            mine = slot(zof(k))
+            line[k] = [send(mine, mine, ss.at[g, k, e], sr.at[g, k, e], peer_of(e)) for e in ring_order(n)]
+
+        zc = {d: send(slot(z), slot(z), zs.at[g, d], zr.at[g, d], dev(dz=d)) for d in z_order[:2]}
+        spread(0)
+        zc.update({d: send(slot(z), slot(z), zs.at[g, d], zr.at[g, d], dev(dz=d)) for d in z_order[2:]})
+        lines = [0] + z_order
+        events = []
+        for s, d in enumerate(z_order):
+            events.append((True, d))
+            if s in (3, 5):
+                events.append((False, lines.pop(0)))
+        events += [(False, k) for k in lines]
+        for s, (first, k) in enumerate(events):
+            hooks(s)
+            if first:
+                zc[k].wait_recv()
+                spread(k)
+            else:
+                for cp in line[k]:
+                    cp.wait_recv()
+                done(zof(k), k)
+
+    TR = min(512, at.shape[1])
+
+    def transpose_part(j, q):
+        if j == q == 0:
+            pltpu.make_async_copy(ab, ab, R["sem_ab"]).wait()
+        t = ab[(j % XN) * 2 + j // XN, q * TR:(q + 1) * TR, :].T
+
+        @pl.when(lax.rem(r, 2) == 0)
+        def _():
+            at[j * BLK:(j + 1) * BLK, q * TR:(q + 1) * TR] = t[:BLK]
+
+        @pl.when(lax.rem(r, 2) == 1)
+        def _():
+            at[j * BLK:(j + 1) * BLK, q * TR:(q + 1) * TR] = t[BLK:]
+
+    fillers = [functools.partial(transpose_part, j, q) for j in range(node_n) for q in range(at.shape[1] // TR)]
+
+    def fill(n):
+        for _ in range(min(n, len(fillers))):
             fillers.pop(0)()
 
-    def transpose_part(j):
-        def run():
-            if j == 0:
-                pltpu.make_async_copy(ab, ab, R["sem_ab"]).wait()
-            t = ab[(j % XN) * 2 + j // XN].T
-
-            @pl.when(lax.rem(r, 2) == 0)
-            def _():
-                at[j * BLK:(j + 1) * BLK, :] = t[:BLK]
-
-            @pl.when(lax.rem(r, 2) == 1)
-            def _():
-                at[j * BLK:(j + 1) * BLK, :] = t[BLK:]
-        return run
-
-    fill = [transpose_part(j) for j in range(node_n)]
+    def fill_hook(s):
+        if s < 8:
+            fill(1)
 
     def unpack_rows(buf, first_block, n, out):
         for k in range(n):
@@ -191,7 +190,7 @@
 
     zacc = R["zacc"]
 
-    def fwd_gather(g, buf, size, prepare, fillers=()):
+    def fwd_gather(g, buf, size, prepare):
         late = []
 
         def line(ck, zk):
@@ -215,20 +214,21 @@
             mine = line(c, zk)
             late.append((send(mine, mine, R["cs"].at[g, k], R["cr"].at[g, k], dev(dc=1)), zk))
             add(c, zk, k == 0)
-            if len(late) > 1:
+            if len(late) > 2:
                 partner()
 
-        gather(g, buf, lambda zk, xk: (c * ZN + zk) * XN + xk, size, XN, x, lambda e: dev(dx=e), done, fillers)
+        gather(g, buf, lambda zk, xk: (c * ZN + zk) * XN + xk, size, XN, x, lambda e: dev(dx=e), done, fill_hook)
         while late:
             partner()
 
-    def fwd_reduce(g, packed):
+    def fwd_reduce(g, packed, n_fill):
         zp, zr = (R["zpp"], R["zrp"]) if packed else (R["zp"], R["zrw"])
         v = zacc[...]
         for k in range(YN):
             piece = v[k * BLK:(k + 1) * BLK]
             zp[k] = pack(piece) if packed else piece
         cps = [send(zp.at[lax.rem(y + e, YN)], zr.at[e], R["rs"].at[g, e], R["rr"].at[g, e], dev(dy=e)) for e in y_order]
+        fill(n_fill)
         total = zp[y]
         for e, cp in zip(y_order, cps):
             cp.wait_recv()
@@ -253,10 +253,10 @@
         unpack_rows(y2g, k * XN, XN, yg.at[1])
 
     mzc = exchange_small(0, mt.at[0], R["mz"], z_order, lambda e: dev(dz=e))
-    fwd_gather(0, xg, BLK, y1_rows, fill[:node_n // 2])
+    fwd_gather(0, xg, BLK, y1_rows)
     small_sum(0, mzc, z_order, R["mz"], 1)
     mxc = exchange_small(1, mt.at[1], R["mx"], x_order, lambda e: dev(dx=e))
-    z1 = fwd_reduce(0, False)
+    z1 = fwd_reduce(0, False, 10)
     R["z1s"][...] = z1
     h1 = jnp.maximum(z1, 0.0).astype(BF)
     R["h1s"][...] = h1
@@ -265,10 +265,10 @@
     y2g[rows(own_f, PB), :] = pack(y2).astype(BF)
     small_sum(1, mxc, x_order, R["mx"], 2)
     myc = exchange_small(2, mt.at[2], R["my"], y_order, lambda e: dev(dy=e))
-    fwd_gather(1, y2g, PB, y2_rows, fill[node_n // 2:])
+    fwd_gather(1, y2g, PB, y2_rows)
     small_sum(2, myc, y_order, R["my"], 3)
     mcc = exchange_small(3, mt.at[3], R["mc"], [1], lambda e: dev(dc=e))
-    z2 = fwd_reduce(1, True)
+    z2 = fwd_reduce(1, True, 99)
     small_sum(3, mcc, [1], R["mc"], 4)
 
     count = mt[4][:1, :1]
@@ -286,7 +286,7 @@
 
     dacc = R["dacc"]
 
-    def bwd(g, buf, size, packed, fillers=()):
+    def bwd(g, buf, size, packed, hooks, late=lambda: None):
         gu = R["gu"] if packed else buf
 
         def done(zk, k):
@@ -299,7 +299,7 @@
             else:
                 dacc[...] += v
 
-        gather(g, buf, lambda zk, yk: zk * YN + yk, size, YN, y, lambda e: dev(dy=e), done, fillers)
+        gather(g, buf, lambda zk, yk: zk * YN + yk, size, YN, y, lambda e: dev(dy=e), done, hooks)
         dp, dr, dsum, dx = (R["dpp"], R["drp"], R["dsp"], R["dxp"]) if packed else (R["dp"], R["dr"], R["ds"], R["dx"])
         for k in range(2):
             for j in range(XN):
@@ -309,78 +309,65 @@
         cp.wait_recv()
         dsum[...] = dp[c] + dr[...]
         cps = [send(dsum.at[lax.rem(x + e, XN)], dx.at[e], R["rs"].at[g, e], R["rr"].at[g, e], dev(dx=e)) for e in x_order]
+        late()
         total = dsum[x]
         for e, cp in zip(x_order, cps):
             cp.wait_recv()
             total = total + dx[e]
         return (unpack(total) if packed else total).astype(BF)
 
-    def all_reduce(t, pay, payd, payx, payy, payz, fin):
-        n_rows = pay.shape[0]
-        rx = n_rows // node_n
+    def all_reduce(t, pay, payx, payy, payz, fin):
+        rx = pay.shape[0] // node_n
         ry = rx // YN
-        half = XN * rx
         fs, fr = R["fs"], R["fr"]
         state = {}
-        base = (c * XN + x) * rx
+        others = range(1, node_n)
+        small = pl.ds(pl.multiple_of(i * rx + y * ry, 8), ry)
+
+        def total(first, buf, order):
+            for e, cp in zip(order, state["cp"]):
+                cp.wait_recv()
+                first = first + buf[e]
+            return first
 
         def s0():
-            state["cp"] = [send(pay.at[rows(1 - c, half)], payd, fs.at[t, 0, 0], fr.at[t, 0, 0], dev(dc=1))]
+            state["cp"] = [send(pay.at[rows(lax.rem(i + e, node_n), rx)], payx.at[e], fs.at[t, 0, e], fr.at[t, 0, e], node_dev(e)) for e in others]
 
         def s1():
-            state["cp"][0].wait_recv()
-            payd[...] = payd[...] + pay[rows(c, half)]
-            state["cp"] = [send(payd.at[rows(lax.rem(x + e, XN), rx)], payx.at[e], fs.at[t, 1, e], fr.at[t, 1, e], dev(dx=e)) for e in x_order]
+            payx[0] = total(pay[rows(i, rx)], payx, others)
+            state["cp"] = [send(payx.at[0, rows(lax.rem(y + e, YN), ry)], payy.at[e], fs.at[t, 1, e], fr.at[t, 1, e], dev(dy=e)) for e in y_order]
 
         def s2():
-            s = payd[rows(x, rx)]
-            for e, cp in zip(x_order, state["cp"]):
-                cp.wait_recv()
-                s = s + payx[e]
-            payx[0] = s
-            state["cp"] = [send(payx.at[0, rows(lax.rem(y + e, YN), ry)], payy.at[e], fs.at[t, 2, e], fr.at[t, 2, e], dev(dy=e)) for e in y_order]
+            payz[z] = total(payx[0, rows(y, ry)], payy, y_order)
+            state["cp"] = [send(payz.at[z], payz.at[z], fs.at[t, 2, d], fr.at[t, 2, d], dev(dz=d)) for d in z_order]
 
         def s3():
-            s = payx[0, rows(y, ry)]
-            for e, cp in zip(y_order, state["cp"]):
-                cp.wait_recv()
-                s = s + payy[e]
-            payz[z] = s
-            state["cp"] = [send(payz.at[z], payz.at[z], fs.at[t, 3, d], fr.at[t, 3, d], dev(dz=d)) for d in z_order]
-
-        def s4():
             for cp in state["cp"]:
                 cp.wait_recv()
             s = payz[0]
             for k in range(1, ZN):
                 s = s + payz[k]
-            mine = fin.at[pl.ds(pl.multiple_of(base + y * ry, 8), ry)]
-            fin[pl.ds(pl.multiple_of(base + y * ry, 8), ry)] = s
-            state["cp"] = [send(mine, mine, fs.at[t, 4, e], fr.at[t, 4, e], dev(dy=e)) for e in y_order]
+            fin[small] = s
+            state["cp"] = [send(fin.at[small], fin.at[small], fs.at[t, 3, e], fr.at[t, 3, e], dev(dy=e)) for e in y_order]
+
+        def s4():
+            for cp in state["cp"]:
+                cp.wait_recv()
+            mine = fin.at[rows(i, rx)]
+            state["cp"] = [send(mine, mine, fs.at[t, 4, e], fr.at[t, 4, e], node_dev(e)) for e in others]
 
         def s5():
             for cp in state["cp"]:
                 cp.wait_recv()
-            mine = fin.at[pl.ds(pl.multiple_of(base, 8), rx)]
-            state["cp"] = [send(mine, mine, fs.at[t, 5, e], fr.at[t, 5, e], dev(dx=e)) for e in x_order]
-
-        def s6():
-            for cp in state["cp"]:
-                cp.wait_recv()
-            mine = fin.at[rows(c, half)]
-            state["cp"] = [send(mine, mine, fs.at[t, 6, 0], fr.at[t, 6, 0], dev(dc=1))]
-
-        def s7():
-            state["cp"][0].wait_recv()
-
-        return [s0, s1, s2, s3, s4, s5, s6, s7]
-
-    d2 = bwd(2, g2g, PB, True)
+
+        return [s0, s1, s2, s3, s4, s5]
+
+    d2 = bwd(2, g2g, PB, True, lambda s: None)
     tn = (((0,), (0,)), ((), ()))
     dh1 = jnp.dot(d2, w2p[...], preferred_element_type=F32)
     g1g[rows(r, BLK), :] = jnp.where(R["z1s"][...] > 0, dh1, 0.0).astype(BF)
     R["d2s"][...] = d2
-    ar2 = all_reduce(0, R["pay2"], R["payd2"], R["payx2"], R["payy2"], R["payz2"], R["fin2"])
+    ar2 = all_reduce(0, R["pay2"], R["payx2"], R["payy2"], R["payz2"], R["fin2"])
 
     def make_dw2():
         dw2 = lax.dot_general(R["d2s"][...], R["h1s"][...], tn, preferred_element_type=F32)
@@ -390,18 +377,24 @@
         R["pay2"][256:512] = dw2[:, 128:]
         ar2[0]()
 
-    def nothing():
-        pass
-
-    d1 = bwd(3, g1g, BLK, False, [make_dw2, nothing, ar2[1], nothing, ar2[2], nothing, ar2[3]])
+    beside = {0: make_dw2, 8: ar2[1], 11: ar2[2]}
+    n_ev = 2 * ZN - 1
+
+    def beside_hook(s):
+        for k in sorted(beside):
+            if k == s or (s == n_ev - 1 and k > s):
+                beside[k]()
+
+    d1 = bwd(3, g1g, BLK, False, beside_hook, ar2[3])
     dw1 = lax.dot_general(x_ref[...], d1, tn, preferred_element_type=F32)
     R["pay1"][0:f_in] = dw1[:, :128]
     R["pay1"][f_in:2 * f_in] = dw1[:, 128:]
-    ar1 = all_reduce(1, R["pay1"], R["payd1"], R["payx1"], R["payy1"], R["payz1"], R["fin1"])
-    for s in range(8):
+    ar1 = all_reduce(1, R["pay1"], R["payx1"], R["payy1"], R["payz1"], R["fin1"])
+    for s in range(6):
         ar1[s]()
-        if s < 4:
-            ar2[4 + s]()
+        if s == 1:
+            ar2[4]()
+    ar2[5]()
     fin1, fin2 = R["fin1"], R["fin2"]
     R["dw2"][:, :128] = fin2[0:classes]
     R["dw2"][:, 128:] = fin2[256:256 + classes]
@@ -428,7 +421,7 @@
 
         def reduce_bufs(t, n):
             rx = n // node_n
-            return {f"pay{t}": V((n, 128), F32), f"payd{t}": V((n // 2, 128), F32), f"payx{t}": V((XN, rx, 128), F32),
+            return {f"pay{t}": V((n, 128), F32), f"payx{t}": V((node_n, rx, 128), F32),
                     f"payy{t}": V((YN, rx // YN, 128), F32), f"payz{t}": V((ZN, rx // YN, 128), F32), f"fin{t}": V((n, 128), F32)}
 
         scratch = dict(

time: 175 us -> 125 us (0.71)
  Pallas kernels: 168 us -> 119 us
    pallas_call x1, Pallas kernels: 168 us -> 119 us  [local_step(): pl.pallas_call(functools.partial(step_kernel, ZN, YN, XN, names), out_sha...]
where the time goes in v3:
time: 125 us
  Pallas kernels  119 us (95%)
  local copies, waits for them, and re-layouts  3.17 us (3%)
  between operations  2.46 us (2%)
    pallas_call x1, Pallas kernels, local_step(): pl.pallas_call(functools.partial(step_kernel, ZN, YN, XN, names), out_sha...  119 us
    unnamed x2, local copies, waits for them, and re-layouts  3.17 us

profile of v3, /device:TPU:1, one launch (start us, length us, event | category | flops | bytes accessed | tf_op | source)
XLA Modules:
  0.0 124.6 jit_solution(16556387993981675360)
XLA Ops:
  0.6 119.0 %gcn_step.1 = (f32[1,1]{1,0:T(1,128)}, f32[128,256]{1,0:T(8,128)}, f32[172,256]{1,0:T(8,128)}) custom-call(bf16[2048,16384]{1,0:T(8,128)(2,1)} %refs_0_.1, bf16[64,128]{1,0:T(8,128)(2,1)} %refs_1_.1, f32[128,256]{1,0:T(8,128)} %refs_2_.1, f32[172,256]{1,0:T(8,128)} %bitcast.6, s32[1,64]{1,0:T(1,128)} %bitcast.7, s32[1,64]{1,0:T(1,128)} %bitcast.8), custom_call_target="tpu_custom_call" | custom-call | tf_op jit(solution)/shard_map/gcn_step/pallas_call | solution.py:447
  120.3 1.6 %copy.13 = f32[128,256]{1,0:T(8,128)} copy(f32[128,256]{1,0:T(8,128)} %get-tuple-element.13) | data formatting | bytes 262144
  121.9 1.6 %copy.14 = f32[256,172]{0,1:T(8,128)} copy(f32[256,172]{0,1:T(8,128)} %bitcast.5) | data formatting | bytes 352256

commit v4 on v3

--- a/solution.py
+++ b/solution.py
@@ -67,12 +67,6 @@
             a_hbm.at[rows(z, rows_z), pl.ds(pl.multiple_of(q * (YN * BLK) + (y // 2) * 128, 128), 128)],
             af.at[:, rows(q, 128)], R["sem_af"]).start()
 
-    @pl.loop(0, node_n)
-    def _(j):
-        pltpu.make_async_copy(
-            a_hbm.at[:, pl.ds(pl.multiple_of(j * (rep_n * BLK) + (r // 2) * 128, 128), 128)],
-            ab.at[j], R["sem_ab"]).start()
-
     barrier = pltpu.get_barrier_semaphore()
     for peer in peers:
         pl.semaphore_signal(barrier, inc=1, device_id=peer, device_id_type=pl.DeviceIdType.MESH)
@@ -86,31 +80,13 @@
     mask_row = R["msk"][...].astype(F32)
     mt[0] = jnp.broadcast_to(jnp.sum(mask_row, axis=1, keepdims=True), mt.shape[1:])
 
-    pltpu.make_async_copy(af, af, R["sem_af"]).wait()
-
-    def select(lo):
-        @pl.loop(0, n_q // 8)
-        def _(step):
-            for u in range(4):
-                p = step * 4 + u
-                xp = lax.rem(p, XN // 2)
-                zk = lax.rem(p // (XN // 2), ZN)
-                ck = p // (XN // 2 * ZN)
-                q = (4 * xp + ck) * ZN + zk
-                even, odd = af[:, rows(q, 128)], af[:, rows(q + 2 * ZN, 128)]
-                ac[:, rows(p, 128)] = jnp.concatenate([even[:, lo:lo + BLK], odd[:, lo:lo + BLK]], axis=1)
-
-    @pl.when(lax.rem(y, 2) == 0)
-    def _():
-        select(0)
-
-    @pl.when(lax.rem(y, 2) == 1)
-    def _():
-        select(BLK)
-
     pl.semaphore_wait(barrier, len(peers))
 
     pending = []
+
+    def drain(keep):
+        while len(pending) > keep:
+            pending.pop(0).wait_send()
 
     def send(src, dst, ssem, rsem, device):
         cp = pltpu.make_async_remote_copy(src_ref=src, dst_ref=dst, send_sem=ssem, recv_sem=rsem,
@@ -119,7 +95,7 @@
         pending.append(cp)
         return cp
 
-    def gather(g, buf, index, size, n, me, peer_of, done, hooks):
+    def gather(g, buf, index, size, n, me, peer_of, done, hooks, z_ahead=False):
         zs, zr, ss, sr = R["zs"], R["zr"], R["ss"], R["sr"]
 
         def slot(zk):
@@ -141,7 +117,7 @@
         events = []
         for s, d in enumerate(z_order):
             events.append((True, d))
-            if s in (3, 5):
+            if s in (3, 5) and not z_ahead:
                 events.append((False, lines.pop(0)))
         events += [(False, k) for k in lines]
         for s, (first, k) in enumerate(events):
@@ -154,6 +130,40 @@
                     cp.wait_recv()
                 done(zof(k), k)
 
+    def select(p, lo):
+        xp, zk, ck = p % (XN // 2), p // (XN // 2) % ZN, p // (XN // 2 * ZN)
+        q = (4 * xp + ck) * ZN + zk
+        even, odd = af[:, q * 128:(q + 1) * 128], af[:, (q + 2 * ZN) * 128:(q + 2 * ZN + 1) * 128]
+        ac[:, p * 128:(p + 1) * 128] = jnp.concatenate([even[:, lo:lo + BLK], odd[:, lo:lo + BLK]], axis=1)
+
+    n_sel = n_q // 2
+
+    def select_hook(s):
+        if s == 0:
+            pltpu.make_async_copy(af, af, R["sem_af"]).wait()
+            start_ab()
+        steps = ZN - 1
+        if s >= steps:
+            return
+        todo = range(s * n_sel // steps, (s + 1) * n_sel // steps)
+
+        @pl.when(lax.rem(y, 2) == 0)
+        def _():
+            for p in todo:
+                select(p, 0)
+
+        @pl.when(lax.rem(y, 2) == 1)
+        def _():
+            for p in todo:
+                select(p, BLK)
+
+    def start_ab():
+        @pl.loop(0, node_n)
+        def _(j):
+            pltpu.make_async_copy(
+                a_hbm.at[:, pl.ds(pl.multiple_of(j * (rep_n * BLK) + (r // 2) * 128, 128), 128)],
+                ab.at[j], R["sem_ab"]).start()
+
     TR = min(512, at.shape[1])
 
     def transpose_part(j, q):
@@ -190,7 +200,7 @@
 
     zacc = R["zacc"]
 
-    def fwd_gather(g, buf, size, prepare):
+    def fwd_gather(g, buf, size, prepare, hooks, z_ahead):
         late = []
 
         def line(ck, zk):
@@ -217,7 +227,7 @@
             if len(late) > 2:
                 partner()
 
-        gather(g, buf, lambda zk, xk: (c * ZN + zk) * XN + xk, size, XN, x, lambda e: dev(dx=e), done, fill_hook)
+        gather(g, buf, lambda zk, xk: (c * ZN + zk) * XN + xk, size, XN, x, lambda e: dev(dx=e), done, hooks, z_ahead)
         while late:
             partner()
 
@@ -229,6 +239,7 @@
             zp[k] = pack(piece) if packed else piece
         cps = [send(zp.at[lax.rem(y + e, YN)], zr.at[e], R["rs"].at[g, e], R["rr"].at[g, e], dev(dy=e)) for e in y_order]
         fill(n_fill)
+        drain(len(cps))
         total = zp[y]
         for e, cp in zip(y_order, cps):
             cp.wait_recv()
@@ -253,10 +264,10 @@
         unpack_rows(y2g, k * XN, XN, yg.at[1])
 
     mzc = exchange_small(0, mt.at[0], R["mz"], z_order, lambda e: dev(dz=e))
-    fwd_gather(0, xg, BLK, y1_rows)
+    fwd_gather(0, xg, BLK, y1_rows, select_hook, True)
     small_sum(0, mzc, z_order, R["mz"], 1)
     mxc = exchange_small(1, mt.at[1], R["mx"], x_order, lambda e: dev(dx=e))
-    z1 = fwd_reduce(0, False, 10)
+    z1 = fwd_reduce(0, False, 14)
     R["z1s"][...] = z1
     h1 = jnp.maximum(z1, 0.0).astype(BF)
     R["h1s"][...] = h1
@@ -265,7 +276,7 @@
     y2g[rows(own_f, PB), :] = pack(y2).astype(BF)
     small_sum(1, mxc, x_order, R["mx"], 2)
     myc = exchange_small(2, mt.at[2], R["my"], y_order, lambda e: dev(dy=e))
-    fwd_gather(1, y2g, PB, y2_rows)
+    fwd_gather(1, y2g, PB, y2_rows, fill_hook, False)
     small_sum(2, myc, y_order, R["my"], 3)
     mcc = exchange_small(3, mt.at[3], R["mc"], [1], lambda e: dev(dc=e))
     z2 = fwd_reduce(1, True, 99)
@@ -310,6 +321,7 @@
         dsum[...] = dp[c] + dr[...]
         cps = [send(dsum.at[lax.rem(x + e, XN)], dx.at[e], R["rs"].at[g, e], R["rr"].at[g, e], dev(dx=e)) for e in x_order]
         late()
+        drain(len(cps) + 3)
         total = dsum[x]
         for e, cp in zip(x_order, cps):
             cp.wait_recv()
@@ -377,24 +389,19 @@
         R["pay2"][256:512] = dw2[:, 128:]
         ar2[0]()
 
-    beside = {0: make_dw2, 8: ar2[1], 11: ar2[2]}
-    n_ev = 2 * ZN - 1
-
     def beside_hook(s):
-        for k in sorted(beside):
-            if k == s or (s == n_ev - 1 and k > s):
-                beside[k]()
-
-    d1 = bwd(3, g1g, BLK, False, beside_hook, ar2[3])
+        if s == 0:
+            make_dw2()
+
+    d1 = bwd(3, g1g, BLK, False, beside_hook, ar2[1])
     dw1 = lax.dot_general(x_ref[...], d1, tn, preferred_element_type=F32)
     R["pay1"][0:f_in] = dw1[:, :128]
     R["pay1"][f_in:2 * f_in] = dw1[:, 128:]
     ar1 = all_reduce(1, R["pay1"], R["payx1"], R["payy1"], R["payz1"], R["fin1"])
     for s in range(6):
         ar1[s]()
-        if s == 1:
-            ar2[4]()
-    ar2[5]()
+        if s < 4:
+            ar2[2 + s]()
     fin1, fin2 = R["fin1"], R["fin2"]
     R["dw2"][:, :128] = fin2[0:classes]
     R["dw2"][:, 128:] = fin2[256:256 + classes]

time: 125 us -> 124 us (level)
  no operation moved by 1% of the time
where the time goes in v4:
time: 124 us
  Pallas kernels  118 us (95%)
  local copies, waits for them, and re-layouts  3.17 us (3%)
  between operations  2.46 us (2%)
    pallas_call x1, Pallas kernels, local_step(): pl.pallas_call(functools.partial(step_kernel, ZN, YN, XN, names), out_sha...  118 us
    unnamed x2, local copies, waits for them, and re-layouts  3.17 us

profile of v4, /device:TPU:1, one launch (start us, length us, event | category | flops | bytes accessed | tf_op | source)
XLA Modules:
  0.0 123.8 jit_solution(9532357279405111923)
XLA Ops:
  0.6 118.2 %gcn_step.1 = (f32[1,1]{1,0:T(1,128)}, f32[128,256]{1,0:T(8,128)}, f32[172,256]{1,0:T(8,128)}) custom-call(bf16[2048,16384]{1,0:T(8,128)(2,1)} %refs_0_.1, bf16[64,128]{1,0:T(8,128)(2,1)} %refs_1_.1, f32[128,256]{1,0:T(8,128)} %refs_2_.1, f32[172,256]{1,0:T(8,128)} %bitcast.6, s32[1,64]{1,0:T(1,128)} %bitcast.7, s32[1,64]{1,0:T(1,128)} %bitcast.8), custom_call_target="tpu_custom_call" | custom-call | tf_op jit(solution)/shard_map/gcn_step/pallas_call | solution.py:454
  119.5 1.6 %copy.13 = f32[128,256]{1,0:T(8,128)} copy(f32[128,256]{1,0:T(8,128)} %get-tuple-element.13) | data formatting | bytes 262144
  121.1 1.6 %copy.14 = f32[256,172]{0,1:T(8,128)} copy(f32[256,172]{0,1:T(8,128)} %bitcast.5) | data formatting | bytes 352256

commit v5 on v4

--- a/solution.py
+++ b/solution.py
@@ -36,7 +36,7 @@
 def step_kernel(ZN, YN, XN, names, *refs):
     R = dict(zip(names, refs))
     a_hbm, x_ref, w1_ref, w2_ref = R["a"], R["x"], R["w1"], R["w2"]
-    af, ac, ab, at, w2p, mt = R["af"], R["ac"], R["ab"], R["at"], R["w2p"], R["mt"]
+    af, ab, at, w2p, mt = R["af"], R["ab"], R["at"], R["w2p"], R["mt"]
     rep_n, node_n = ZN * YN, 2 * XN
     r, i = lax.axis_index("rep"), lax.axis_index("nodes")
     z, y = r // YN, lax.rem(r, YN)
@@ -65,7 +65,7 @@
     def _(q):
         pltpu.make_async_copy(
             a_hbm.at[rows(z, rows_z), pl.ds(pl.multiple_of(q * (YN * BLK) + (y // 2) * 128, 128), 128)],
-            af.at[:, rows(q, 128)], R["sem_af"]).start()
+            af.at[:, rows((lax.rem(q // ZN, 2) * ZN + lax.rem(q, ZN)) * XN + q // (2 * ZN), 128)], R["sem_af"]).start()
 
     barrier = pltpu.get_barrier_semaphore()
     for peer in peers:
@@ -74,6 +74,14 @@
     xg, yg, y2g, g2g, g1g = R["xg"], R["yg"], R["y2g"], R["g2g"], R["g1g"]
     own_f = (c * ZN + z) * XN + x
     xg[rows(own_f, BLK), :] = x_ref[...]
+    mine_at = lax.rem(y, 2) * BLK
+
+    @pl.loop(0, yg.shape[1] // 128)
+    def _(k):
+        zero_rows = pl.ds(pl.multiple_of(k * 128 + BLK - mine_at, BLK), BLK)
+        for t in range(2):
+            yg[t, zero_rows, :] = jnp.zeros((BLK, 256), BF)
+
     w2p[...] = jnp.zeros_like(w2p)
     w2p[:classes, :] = w2_ref[...].astype(BF)
     b1 = w1_ref[...].astype(BF)
@@ -130,33 +138,6 @@
                     cp.wait_recv()
                 done(zof(k), k)
 
-    def select(p, lo):
-        xp, zk, ck = p % (XN // 2), p // (XN // 2) % ZN, p // (XN // 2 * ZN)
-        q = (4 * xp + ck) * ZN + zk
-        even, odd = af[:, q * 128:(q + 1) * 128], af[:, (q + 2 * ZN) * 128:(q + 2 * ZN + 1) * 128]
-        ac[:, p * 128:(p + 1) * 128] = jnp.concatenate([even[:, lo:lo + BLK], odd[:, lo:lo + BLK]], axis=1)
-
-    n_sel = n_q // 2
-
-    def select_hook(s):
-        if s == 0:
-            pltpu.make_async_copy(af, af, R["sem_af"]).wait()
-            start_ab()
-        steps = ZN - 1
-        if s >= steps:
-            return
-        todo = range(s * n_sel // steps, (s + 1) * n_sel // steps)
-
-        @pl.when(lax.rem(y, 2) == 0)
-        def _():
-            for p in todo:
-                select(p, 0)
-
-        @pl.when(lax.rem(y, 2) == 1)
-        def _():
-            for p in todo:
-                select(p, BLK)
-
     def start_ab():
         @pl.loop(0, node_n)
         def _(j):
@@ -189,10 +170,10 @@
         if s < 8:
             fill(1)
 
-    def unpack_rows(buf, first_block, n, out):
+    def unpack_rows(buf, first_block, n, out, pitch=BLK, shift=0):
         for k in range(n):
             base = pl.multiple_of((first_block + k) * PB, 32)
-            orow = pl.multiple_of((first_block + k) * BLK, BLK)
+            orow = pl.multiple_of((first_block + k) * pitch + shift, BLK)
             t = buf[pl.ds(base + BLK, BLK // 2), :]
             out[pl.ds(orow, BLK), :128] = buf[pl.ds(base, BLK), :]
             out[pl.ds(orow, BLK // 2), 128:] = t
@@ -208,8 +189,11 @@
 
         def add(ck, zk, first):
             k = ck * ZN + zk
+            if first and g == 0:
+                pltpu.make_async_copy(af, af, R["sem_af"]).wait()
+                start_ab()
             prepare(k)
-            v = jnp.dot(ac[:, rows(k, XN * BLK)], yg[g, rows(k, XN * BLK), :], preferred_element_type=F32)
+            v = jnp.dot(af[:, rows(k, XN * 128)], yg[g, rows(k, XN * 128), :], preferred_element_type=F32)
             if first:
                 zacc[...] = v
             else:
@@ -258,13 +242,15 @@
 
     def y1_rows(k):
         rr = rows(k, XN * BLK)
-        yg[0, rr, :] = jnp.dot(xg[rr, :], b1, preferred_element_type=F32).astype(BF)
+        v = jnp.dot(xg[rr, :], b1, preferred_element_type=F32).astype(BF)
+        for j in range(XN):
+            yg[0, pl.ds(pl.multiple_of((k * XN + j) * 128 + mine_at, BLK), BLK), :] = v[j * BLK:(j + 1) * BLK]
 
     def y2_rows(k):
-        unpack_rows(y2g, k * XN, XN, yg.at[1])
+        unpack_rows(y2g, k * XN, XN, yg.at[1], 128, mine_at)
 
     mzc = exchange_small(0, mt.at[0], R["mz"], z_order, lambda e: dev(dz=e))
-    fwd_gather(0, xg, BLK, y1_rows, select_hook, True)
+    fwd_gather(0, xg, BLK, y1_rows, lambda s: None, False)
     small_sum(0, mzc, z_order, R["mz"], 1)
     mxc = exchange_small(1, mt.at[1], R["mx"], x_order, lambda e: dev(dx=e))
     z1 = fwd_reduce(0, False, 14)
@@ -328,7 +314,7 @@
             total = total + dx[e]
         return (unpack(total) if packed else total).astype(BF)
 
-    def all_reduce(t, pay, payx, payy, payz, fin):
+    def all_reduce(t, pay, payx, payy, payz, fin, whole):
         rx = pay.shape[0] // node_n
         ry = rx // YN
         fs, fr = R["fs"], R["fr"]
@@ -344,6 +330,27 @@
 
         def s0():
             state["cp"] = [send(pay.at[rows(lax.rem(i + e, node_n), rx)], payx.at[e], fs.at[t, 0, e], fr.at[t, 0, e], node_dev(e)) for e in others]
+
+        def w1():
+            payy[y] = total(pay[rows(i, rx)], payx, others)
+            state["cp"] = [send(payy.at[y], payy.at[y], fs.at[t, 1, e], fr.at[t, 1, e], dev(dy=e)) for e in y_order]
+
+        def in_order(buf, n):
+            for cp in state["cp"]:
+                cp.wait_recv()
+            s = buf[0]
+            for k in range(1, n):
+                s = s + buf[k]
+            return s
+
+        def w2():
+            payz[z] = in_order(payy, YN)
+            state["cp"] = [send(payz.at[z], payz.at[z], fs.at[t, 2, d], fr.at[t, 2, d], dev(dz=d)) for d in z_order]
+
+        def w3():
+            fin[rows(i, rx)] = in_order(payz, ZN)
+            mine = fin.at[rows(i, rx)]
+            state["cp"] = [send(mine, mine, fs.at[t, 4, e], fr.at[t, 4, e], node_dev(e)) for e in others]
 
         def s1():
             payx[0] = total(pay[rows(i, rx)], payx, others)
@@ -372,14 +379,14 @@
             for cp in state["cp"]:
                 cp.wait_recv()
 
-        return [s0, s1, s2, s3, s4, s5]
+        return [s0, w1, w2, w3, s5] if whole else [s0, s1, s2, s3, s4, s5]
 
     d2 = bwd(2, g2g, PB, True, lambda s: None)
     tn = (((0,), (0,)), ((), ()))
     dh1 = jnp.dot(d2, w2p[...], preferred_element_type=F32)
     g1g[rows(r, BLK), :] = jnp.where(R["z1s"][...] > 0, dh1, 0.0).astype(BF)
     R["d2s"][...] = d2
-    ar2 = all_reduce(0, R["pay2"], R["payx2"], R["payy2"], R["payz2"], R["fin2"])
+    ar2 = all_reduce(0, R["pay2"], R["payx2"], R["payy2"], R["payz2"], R["fin2"], False)
 
     def make_dw2():
         dw2 = lax.dot_general(R["d2s"][...], R["h1s"][...], tn, preferred_element_type=F32)
@@ -397,19 +404,25 @@
     dw1 = lax.dot_general(x_ref[...], d1, tn, preferred_element_type=F32)
     R["pay1"][0:f_in] = dw1[:, :128]
     R["pay1"][f_in:2 * f_in] = dw1[:, 128:]
-    ar1 = all_reduce(1, R["pay1"], R["payx1"], R["payy1"], R["payz1"], R["fin1"])
-    for s in range(6):
+    ar1 = all_reduce(1, R["pay1"], R["payx1"], R["payy1"], R["payz1"], R["fin1"], True)
+    for s in range(5):
         ar1[s]()
         if s < 4:
             ar2[2 + s]()
-    fin1, fin2 = R["fin1"], R["fin2"]
-    R["dw2"][:, :128] = fin2[0:classes]
-    R["dw2"][:, 128:] = fin2[256:256 + classes]
-    R["loss"][0, 0] = jnp.sum(fin2[255:256, 127:] / count)
-    R["dw1"][:, :128] = fin1[0:f_in]
-    R["dw1"][:, 128:] = fin1[f_in:2 * f_in]
+    R["o1"][...] = R["fin1"][...]
+    R["o2"][...] = R["fin2"][...]
+    R["cnt"][...] = mt[4]
     for cp in pending:
         cp.wait_send()
+
+
+def write_outputs(fin1, fin2, count, loss_ref, dw1_ref, dw2_ref):
+    f_in, classes = dw1_ref.shape[0], dw2_ref.shape[0]
+    dw2_ref[:, :128] = fin2[0:classes]
+    dw2_ref[:, 128:] = fin2[256:256 + classes]
+    loss_ref[0, 0] = jnp.sum(fin2[255:256, 127:] / count[:1, :1])
+    dw1_ref[:, :128] = fin1[0:f_in]
+    dw1_ref[:, 128:] = fin1[f_in:2 * f_in]
 
 
 def solution(mesh):
@@ -426,15 +439,15 @@
         V = pltpu.VMEM
         D = pltpu.SemaphoreType.DMA
 
-        def reduce_bufs(t, n):
+        def reduce_bufs(t, n, cut):
             rx = n // node_n
             return {f"pay{t}": V((n, 128), F32), f"payx{t}": V((node_n, rx, 128), F32),
-                    f"payy{t}": V((YN, rx // YN, 128), F32), f"payz{t}": V((ZN, rx // YN, 128), F32), f"fin{t}": V((n, 128), F32)}
+                    f"payy{t}": V((YN, rx // cut, 128), F32), f"payz{t}": V((ZN, rx // cut, 128), F32), f"fin{t}": V((n, 128), F32)}
 
         scratch = dict(
-            af=V((YN * BLK, blocks_y * 128), BF), ac=V((YN * BLK, blocks_y * BLK), BF),
+            af=V((YN * BLK, blocks_y * 128), BF),
             ab=V((node_n, rows_g, 128), BF), at=V((node_n * BLK, rows_g), BF),
-            xg=V((blocks_y * BLK, f_in), BF), yg=V((2, blocks_y * BLK, 256), BF), y2g=V((blocks_y * 96, 128), BF),
+            xg=V((blocks_y * BLK, f_in), BF), yg=V((2, blocks_y * 128, 256), BF), y2g=V((blocks_y * 96, 128), BF),
             g2g=V((rep_n * 96, 128), BF), gu=V((rows_g, 256), BF), g1g=V((rows_g, hidden), BF),
             zacc=V((YN * BLK, 256), F32), dacc=V((node_n * BLK, 256), F32),
             zp=V((YN, BLK, 256), F32), zrw=V((YN, BLK, 256), F32), zpp=V((YN, 96, 128), F32), zrp=V((YN, 96, 128), F32),
@@ -447,20 +460,28 @@
             zs=D((4, 8)), zr=D((4, 8)), ss=D((4, 8, 4)), sr=D((4, 8, 4)), cs=D((4, 8)), cr=D((4, 8)),
             rs=D((4, 4)), rr=D((4, 4)), ms=D((4, 8)), mr=D((4, 8)), fs=D((2, 7, 8)), fr=D((2, 7, 8)),
         )
-        scratch.update(reduce_bufs(1, 2 * f_in))
-        scratch.update(reduce_bufs(2, 512))
-        names = ["a", "x", "w1", "w2", "lab", "msk", "loss", "dw1", "dw2"] + list(scratch)
+        scratch.update(reduce_bufs(1, 2 * f_in, 1))
+        scratch.update(reduce_bufs(2, 512, YN))
+        names = ["a", "x", "w1", "w2", "lab", "msk", "o1", "o2", "cnt"] + list(scratch)
         vm = pl.BlockSpec(memory_space=pltpu.VMEM)
-        loss, dw1, dw2 = pl.pallas_call(
+        sums = pl.pallas_call(
             functools.partial(step_kernel, ZN, YN, XN, names),
-            out_shape=(jax.ShapeDtypeStruct((1, 1), F32), jax.ShapeDtypeStruct((f_in, hidden), F32),
-                       jax.ShapeDtypeStruct((classes, hidden), F32)),
+            out_shape=(jax.ShapeDtypeStruct((2 * f_in, 128), F32), jax.ShapeDtypeStruct((512, 128), F32),
+                       jax.ShapeDtypeStruct((8, 128), F32)),
             in_specs=[pl.BlockSpec(memory_space=pl.ANY), vm, vm, vm, vm, vm],
-            out_specs=(pl.BlockSpec(memory_space=pltpu.SMEM), vm, vm),
+            out_specs=(vm, vm, vm),
             scratch_shapes=list(scratch.values()),
             compiler_params=pltpu.CompilerParams(collective_id=0, has_side_effects=True, vmem_limit_bytes=60 * 2 ** 20),
             name="gcn_step",
         )(adj, features, w_one, w_two.T, labels.reshape(1, BLK), mask.reshape(1, BLK))
+        loss, dw1, dw2 = pl.pallas_call(
+            write_outputs,
+            out_shape=(jax.ShapeDtypeStruct((1, 1), F32), jax.ShapeDtypeStruct((f_in, hidden), F32),
+                       jax.ShapeDtypeStruct((classes, hidden), F32)),
+            in_specs=[vm, vm, vm],
+            out_specs=(pl.BlockSpec(memory_space=pltpu.SMEM), vm, vm),
+            name="write_outputs",
+        )(*sums)
         return loss.reshape(()), dw1, dw2.T
 
     row_spec = P(("nodes", "rep"))

time: 124 us -> 121 us (0.976)
  local copies, waits for them, and re-layouts: 3.17 us -> 0 us
  Pallas kernels: 118 us -> 120 us
  between operations: 2.46 us -> 0.64 us
    unnamed x2 -> x0, local copies, waits for them, and re-layouts: 3.17 us -> none
    pallas_call x0 -> x1, Pallas kernels: none -> 1.74 us  [local_step(): pl.pallas_call(write_outputs, out_shape=(jax.ShapeDtypeStruct((1, 1), F32...]
where the time goes in v5:
time: 121 us
  Pallas kernels  120 us (99%)
    pallas_call x1, Pallas kernels, local_step(): pl.pallas_call(functools.partial(step_kernel, ZN, YN, XN, names), out_sha...  119 us

profile of v5, /device:TPU:1, one launch (start us, length us, event | category | flops | bytes accessed | tf_op | source)
XLA Modules:
  0.0 121.0 jit_solution(3720869515070132170)
XLA Ops:
  0.6 118.6 %gcn_step.1 = (f32[256,128]{1,0:T(8,128)}, f32[512,128]{1,0:T(8,128)}, f32[8,128]{1,0:T(8,128)}) custom-call(bf16[2048,16384]{1,0:T(8,128)(2,1)} %refs_0_.1, bf16[64,128]{1,0:T(8,128)(2,1)} %refs_1_.1, f32[128,256]{1,0:T(8,128)} %refs_2_.1, f32[172,256]{1,0:T(8,128)} %bitcast.5, s32[1,64]{1,0:T(1,128)} %bitcast.6, s32[1,64]{1,0:T(1,128)} %bitcast.7), custom_call_target="tpu_custom_call" | custom-call | tf_op jit(solution)/shard_map/gcn_step/pallas_call | solution.py:467
  119.2 1.7 %write_outputs.1 = (f32[1,1]{1,0:T(1,128)}, f32[128,256]{1,0:T(8,128)}, f32[172,256]{1,0:T(8,128)}) custom-call(f32[256,128]{1,0:T(8,128)} %get-tuple-element.9.fin1, f32[512,128]{1,0:T(8,128)} %get-tuple-element.10.fin2, f32[8,128]{1,0:T(8,128)} %get-tuple-element.11.count), custom_call_target="tpu_custom_call" | custom-call | tf_op jit(solution)/shard_map/write_outputs/pallas_call | solution.py:477

commit v6 on v5

--- a/solution.py
+++ b/solution.py
@@ -103,7 +103,7 @@
         pending.append(cp)
         return cp
 
-    def gather(g, buf, index, size, n, me, peer_of, done, hooks, z_ahead=False):
+    def gather(g, buf, index, size, n, me, peer_of, done, hooks):
         zs, zr, ss, sr = R["zs"], R["zr"], R["ss"], R["sr"]
 
         def slot(zk):
@@ -113,26 +113,37 @@
             return lax.rem(z + ZN - k, ZN)
 
         line = {}
+        early = [k for k in [0] + z_order if min(k, ZN - k) <= 2] if n == 4 else []
 
         def spread(k):
             mine = slot(zof(k))
-            line[k] = [send(mine, mine, ss.at[g, k, e], sr.at[g, k, e], peer_of(e)) for e in ring_order(n)]
+            line[k] = [send(mine, mine, ss.at[g, k, e], sr.at[g, k, e], peer_of(e))
+                       for e in ring_order(n) if e != 2 or k not in early]
+
+        def relay(k):
+            far = []
+            for h, cp in enumerate(line[k]):
+                cp.wait_recv()
+                at_row = index(zof(k), lax.rem(me + (n - 1 if h == 0 else 1), n)) * size + h * (size // 2)
+                piece = buf.at[pl.ds(pl.multiple_of(at_row, size // 2), size // 2)]
+                far.append(send(piece, piece, ss.at[g, k, 2 * h], sr.at[g, k, 2 * h], peer_of(1 if h == 0 else n - 1)))
+            line[k] = far
 
         zc = {d: send(slot(z), slot(z), zs.at[g, d], zr.at[g, d], dev(dz=d)) for d in z_order[:2]}
         spread(0)
         zc.update({d: send(slot(z), slot(z), zs.at[g, d], zr.at[g, d], dev(dz=d)) for d in z_order[2:]})
-        lines = [0] + z_order
+        after = {1: "r0", 3: "r1 r7", 5: "l0 r2 r6", 6: "l1 l7 l2 l6 l3 l5 l4"} if ZN == 8 else {ZN - 2: "r0 l0 r1 l1"}
         events = []
         for s, d in enumerate(z_order):
-            events.append((True, d))
-            if s in (3, 5) and not z_ahead:
-                events.append((False, lines.pop(0)))
-        events += [(False, k) for k in lines]
-        for s, (first, k) in enumerate(events):
-            hooks(s)
-            if first:
+            events.append(("z", d))
+            events += [(w[0], int(w[1:])) for w in after.get(s, "").split() if w[0] == "l" or int(w[1:]) in early]
+        for s, (what, k) in enumerate(events):
+            hooks(s if what != "r" else 99)
+            if what == "z":
                 zc[k].wait_recv()
                 spread(k)
+            elif what == "r":
+                relay(k)
             else:
                 for cp in line[k]:
                     cp.wait_recv()
@@ -167,7 +178,7 @@
             fillers.pop(0)()
 
     def fill_hook(s):
-        if s < 8:
+        if s < 14:
             fill(1)
 
     def unpack_rows(buf, first_block, n, out, pitch=BLK, shift=0):
@@ -181,7 +192,7 @@
 
     zacc = R["zacc"]
 
-    def fwd_gather(g, buf, size, prepare, hooks, z_ahead):
+    def fwd_gather(g, buf, size, prepare, hooks):
         late = []
 
         def line(ck, zk):
@@ -211,7 +222,7 @@
             if len(late) > 2:
                 partner()
 
-        gather(g, buf, lambda zk, xk: (c * ZN + zk) * XN + xk, size, XN, x, lambda e: dev(dx=e), done, hooks, z_ahead)
+        gather(g, buf, lambda zk, xk: (c * ZN + zk) * XN + xk, size, XN, x, lambda e: dev(dx=e), done, hooks)
         while late:
             partner()
 
@@ -249,11 +260,16 @@
     def y2_rows(k):
         unpack_rows(y2g, k * XN, XN, yg.at[1], 128, mine_at)
 
-    mzc = exchange_small(0, mt.at[0], R["mz"], z_order, lambda e: dev(dz=e))
-    fwd_gather(0, xg, BLK, y1_rows, lambda s: None, False)
+    mzc = []
+
+    def count_hook(s):
+        if s == 0:
+            mzc.extend(exchange_small(0, mt.at[0], R["mz"], z_order, lambda e: dev(dz=e)))
+
+    fwd_gather(0, xg, BLK, y1_rows, count_hook)
     small_sum(0, mzc, z_order, R["mz"], 1)
     mxc = exchange_small(1, mt.at[1], R["mx"], x_order, lambda e: dev(dx=e))
-    z1 = fwd_reduce(0, False, 14)
+    z1 = fwd_reduce(0, False, 12)
     R["z1s"][...] = z1
     h1 = jnp.maximum(z1, 0.0).astype(BF)
     R["h1s"][...] = h1
@@ -262,7 +278,7 @@
     y2g[rows(own_f, PB), :] = pack(y2).astype(BF)
     small_sum(1, mxc, x_order, R["mx"], 2)
     myc = exchange_small(2, mt.at[2], R["my"], y_order, lambda e: dev(dy=e))
-    fwd_gather(1, y2g, PB, y2_rows, fill_hook, False)
+    fwd_gather(1, y2g, PB, y2_rows, fill_hook)
     small_sum(2, myc, y_order, R["my"], 3)
     mcc = exchange_small(3, mt.at[3], R["mc"], [1], lambda e: dev(dc=e))
     z2 = fwd_reduce(1, True, 99)

time: 121 us -> 125 us (1.033)
  Pallas kernels: 120 us -> 124 us
    pallas_call x1, Pallas kernels: 119 us -> 123 us  [local_step(): pl.pallas_call(functools.partial(step_kernel, ZN, YN, XN, names), out_sha...]
where the time goes in v6:
time: 125 us
  Pallas kernels  124 us (99%)
    pallas_call x1, Pallas kernels, local_step(): pl.pallas_call(functools.partial(step_kernel, ZN, YN, XN, names), out_sha...  123 us

profile of v6, /device:TPU:1, one launch (start us, length us, event | category | flops | bytes accessed | tf_op | source)
XLA Modules:
  0.0 125.1 jit_solution(12718197383274588424)
XLA Ops:
  0.6 122.8 %gcn_step.1 = (f32[256,128]{1,0:T(8,128)}, f32[512,128]{1,0:T(8,128)}, f32[8,128]{1,0:T(8,128)}) custom-call(bf16[2048,16384]{1,0:T(8,128)(2,1)} %refs_0_.1, bf16[64,128]{1,0:T(8,128)(2,1)} %refs_1_.1, f32[128,256]{1,0:T(8,128)} %refs_2_.1, f32[172,256]{1,0:T(8,128)} %bitcast.5, s32[1,64]{1,0:T(1,128)} %bitcast.6, s32[1,64]{1,0:T(1,128)} %bitcast.7), custom_call_target="tpu_custom_call" | custom-call | tf_op jit(solution)/shard_map/gcn_step/pallas_call | solution.py:483
  123.4 1.7 %write_outputs.1 = (f32[1,1]{1,0:T(1,128)}, f32[128,256]{1,0:T(8,128)}, f32[172,256]{1,0:T(8,128)}) custom-call(f32[256,128]{1,0:T(8,128)} %get-tuple-element.9.fin1, f32[512,128]{1,0:T(8,128)} %get-tuple-element.10.fin2, f32[8,128]{1,0:T(8,128)} %get-tuple-element.11.count), custom_call_target="tpu_custom_call" | custom-call | tf_op jit(solution)/shard_map/write_outputs/pallas_call | solution.py:493

commit v7 on v5

--- a/solution.py
+++ b/solution.py
@@ -103,7 +103,7 @@
         pending.append(cp)
         return cp
 
-    def gather(g, buf, index, size, n, me, peer_of, done, hooks, z_ahead=False):
+    def gather(g, buf, index, size, n, me, peer_of, done, hooks):
         zs, zr, ss, sr = R["zs"], R["zr"], R["ss"], R["sr"]
 
         def slot(zk):
@@ -125,8 +125,6 @@
         events = []
         for s, d in enumerate(z_order):
             events.append((True, d))
-            if s in (3, 5) and not z_ahead:
-                events.append((False, lines.pop(0)))
         events += [(False, k) for k in lines]
         for s, (first, k) in enumerate(events):
             hooks(s)
@@ -167,8 +165,8 @@
             fillers.pop(0)()
 
     def fill_hook(s):
-        if s < 8:
-            fill(1)
+        if s == 0:
+            fill(4)
 
     def unpack_rows(buf, first_block, n, out, pitch=BLK, shift=0):
         for k in range(n):
@@ -181,7 +179,7 @@
 
     zacc = R["zacc"]
 
-    def fwd_gather(g, buf, size, prepare, hooks, z_ahead):
+    def fwd_gather(g, buf, size, prepare, hooks):
         late = []
 
         def line(ck, zk):
@@ -211,7 +209,7 @@
             if len(late) > 2:
                 partner()
 
-        gather(g, buf, lambda zk, xk: (c * ZN + zk) * XN + xk, size, XN, x, lambda e: dev(dx=e), done, hooks, z_ahead)
+        gather(g, buf, lambda zk, xk: (c * ZN + zk) * XN + xk, size, XN, x, lambda e: dev(dx=e), done, hooks)
         while late:
             partner()
 
@@ -249,11 +247,16 @@
     def y2_rows(k):
         unpack_rows(y2g, k * XN, XN, yg.at[1], 128, mine_at)
 
-    mzc = exchange_small(0, mt.at[0], R["mz"], z_order, lambda e: dev(dz=e))
-    fwd_gather(0, xg, BLK, y1_rows, lambda s: None, False)
+    mzc = []
+
+    def count_hook(s):
+        if s == 0:
+            mzc.extend(exchange_small(0, mt.at[0], R["mz"], z_order, lambda e: dev(dz=e)))
+
+    fwd_gather(0, xg, BLK, y1_rows, count_hook)
     small_sum(0, mzc, z_order, R["mz"], 1)
     mxc = exchange_small(1, mt.at[1], R["mx"], x_order, lambda e: dev(dx=e))
-    z1 = fwd_reduce(0, False, 14)
+    z1 = fwd_reduce(0, False, 12)
     R["z1s"][...] = z1
     h1 = jnp.maximum(z1, 0.0).astype(BF)
     R["h1s"][...] = h1
@@ -262,10 +265,10 @@
     y2g[rows(own_f, PB), :] = pack(y2).astype(BF)
     small_sum(1, mxc, x_order, R["mx"], 2)
     myc = exchange_small(2, mt.at[2], R["my"], y_order, lambda e: dev(dy=e))
-    fwd_gather(1, y2g, PB, y2_rows, fill_hook, False)
+    fwd_gather(1, y2g, PB, y2_rows, fill_hook)
     small_sum(2, myc, y_order, R["my"], 3)
     mcc = exchange_small(3, mt.at[3], R["mc"], [1], lambda e: dev(dc=e))
-    z2 = fwd_reduce(1, True, 99)
+    z2 = fwd_reduce(1, True, 11)
     small_sum(3, mcc, [1], R["mc"], 4)
 
     count = mt[4][:1, :1]
@@ -381,7 +384,7 @@
 
         return [s0, w1, w2, w3, s5] if whole else [s0, s1, s2, s3, s4, s5]
 
-    d2 = bwd(2, g2g, PB, True, lambda s: None)
+    d2 = bwd(2, g2g, PB, True, lambda s: fill(99) if s == 0 else None)
     tn = (((0,), (0,)), ((), ()))
     dh1 = jnp.dot(d2, w2p[...], preferred_element_type=F32)
     g1g[rows(r, BLK), :] = jnp.where(R["z1s"][...] > 0, dh1, 0.0).astype(BF)

time: 121 us -> 120 us (level)
  no operation moved by 1% of the time
where the time goes in v7:
time: 120 us
  Pallas kernels  119 us (99%)
    pallas_call x1, Pallas kernels, local_step(): pl.pallas_call(functools.partial(step_kernel, ZN, YN, XN, names), out_sha...  117 us

profile of v7, /device:TPU:1, one launch (start us, length us, event | category | flops | bytes accessed | tf_op | source)
XLA Modules:
  0.0 119.8 jit_solution(7447439004789278543)
XLA Ops:
  0.6 117.4 %gcn_step.1 = (f32[256,128]{1,0:T(8,128)}, f32[512,128]{1,0:T(8,128)}, f32[8,128]{1,0:T(8,128)}) custom-call(bf16[2048,16384]{1,0:T(8,128)(2,1)} %refs_0_.1, bf16[64,128]{1,0:T(8,128)(2,1)} %refs_1_.1, f32[128,256]{1,0:T(8,128)} %refs_2_.1, f32[172,256]{1,0:T(8,128)} %bitcast.5, s32[1,64]{1,0:T(1,128)} %bitcast.6, s32[1,64]{1,0:T(1,128)} %bitcast.7), custom_call_target="tpu_custom_call" | custom-call | tf_op jit(solution)/shard_map/gcn_step/pallas_call | solution.py:470
  118.0 1.7 %write_outputs.1 = (f32[1,1]{1,0:T(1,128)}, f32[128,256]{1,0:T(8,128)}, f32[172,256]{1,0:T(8,128)}) custom-call(f32[256,128]{1,0:T(8,128)} %get-tuple-element.9.fin1, f32[512,128]{1,0:T(8,128)} %get-tuple-element.10.fin2, f32[8,128]{1,0:T(8,128)} %get-tuple-element.11.count), custom_call_target="tpu_custom_call" | custom-call | tf_op jit(solution)/shard_map/write_outputs/pallas_call | solution.py:480

commit v8 on v7

--- a/solution.py
+++ b/solution.py
@@ -14,6 +14,8 @@
 
 
 def ring_order(n):
+    if n == 4:
+        return [2, 1, 3]
     return sorted(range(1, n), key=lambda d: (min(d, n - d), d))
 
 

time: 120 us -> 118 us (0.983)
  Pallas kernels: 119 us -> 117 us
    pallas_call x1, Pallas kernels: 117 us -> 115 us  [local_step(): pl.pallas_call(functools.partial(step_kernel, ZN, YN, XN, names), out_sha...]
where the time goes in v8:
time: 118 us
  Pallas kernels  117 us (99%)
    pallas_call x1, Pallas kernels, local_step(): pl.pallas_call(functools.partial(step_kernel, ZN, YN, XN, names), out_sha...  115 us

profile of v8, /device:TPU:1, one launch (start us, length us, event | category | flops | bytes accessed | tf_op | source)
XLA Modules:
  0.0 117.8 jit_solution(14076449400259068837)
XLA Ops:
  0.6 115.4 %gcn_step.1 = (f32[256,128]{1,0:T(8,128)}, f32[512,128]{1,0:T(8,128)}, f32[8,128]{1,0:T(8,128)}) custom-call(bf16[2048,16384]{1,0:T(8,128)(2,1)} %refs_0_.1, bf16[64,128]{1,0:T(8,128)(2,1)} %refs_1_.1, f32[128,256]{1,0:T(8,128)} %refs_2_.1, f32[172,256]{1,0:T(8,128)} %bitcast.5, s32[1,64]{1,0:T(1,128)} %bitcast.6, s32[1,64]{1,0:T(1,128)} %bitcast.7), custom_call_target="tpu_custom_call" | custom-call | tf_op jit(solution)/shard_map/gcn_step/pallas_call | solution.py:472
  116.1 1.7 %write_outputs.1 = (f32[1,1]{1,0:T(1,128)}, f32[128,256]{1,0:T(8,128)}, f32[172,256]{1,0:T(8,128)}) custom-call(f32[256,128]{1,0:T(8,128)} %get-tuple-element.9.fin1, f32[512,128]{1,0:T(8,128)} %get-tuple-element.10.fin2, f32[8,128]{1,0:T(8,128)} %get-tuple-element.11.count), custom_call_target="tpu_custom_call" | custom-call | tf_op jit(solution)/shard_map/write_outputs/pallas_call | solution.py:482
